TPU v7x, 128 devices: a whole 4x4x4 slice. The times are simulated.
128 devices in a mesh: dp: 1, sp: 128 (over z, y, x, core).
Axes of the slice: x: 4, y: 4, z: 4, core: 2. Of those that a mesh axis runs over, the one named last changes fastest.
Arguments:
- tokens: bfloat16 [64, 2560], P('dp')
- positions: int32 [64], P('dp')
- k_cache: bfloat16 [64, 2048, 8, 128], P('dp', 'sp')
- v_cache: bfloat16 [64, 2048, 8, 128], P('dp', 'sp')
- w_q: bfloat16 [2560, 4096], replicated
- w_k: bfloat16 [2560, 1024], replicated
- w_v: bfloat16 [2560, 1024], replicated
- w_o: bfloat16 [4096, 2560], replicated
- attn_norm: bfloat16 [2560], replicated
- q_norm: bfloat16 [128], replicated
- k_norm: bfloat16 [128], replicated
Outputs:
- output 1: bfloat16 [64, 2560], P('dp')
- output 2: bfloat16 [64, 2048, 8, 128], P('dp', 'sp')
- output 3: bfloat16 [64, 2048, 8, 128], P('dp', 'sp')
- output 4: bfloat16 [64, 2, 8, 128], P('dp')
All inputs are finite; a program needn't handle non-finite values.
Results may differ from a plain program's by a relative error of at most 0.00652824.
Values sent between devices are 32-bit elements.
A program may use at most 1 GiB of HBM per device.

v0:
```python
import jax
import jax.numpy as jnp
from jax import lax
from jax.sharding import PartitionSpec as P

NORM_EPS = 1e-6
ROPE_THETA = 1000000.0
NEG_FILL = -1e30


def rms_scale(values, gain):
    return values * lax.rsqrt(jnp.mean(values * values, axis=-1, keepdims=True) + NORM_EPS) * gain.astype(jnp.float32)


def rope_table(positions, head_dim):
    inv_freq = ROPE_THETA ** (-jnp.arange(head_dim // 2, dtype=jnp.float32) * 2.0 / head_dim)
    angles = positions.astype(jnp.float32)[:, None] * inv_freq[None, :]
    return jnp.cos(angles)[:, None, :], jnp.sin(angles)[:, None, :]


def norm_rope(proj, gain, cos_table, sin_table):
    normed = rms_scale(proj.astype(jnp.float32), gain)
    half_dim = proj.shape[-1] // 2
    first_half = normed[..., :half_dim]
    second_half = normed[..., half_dim:]
    rotated = jnp.concatenate([first_half * cos_table - second_half * sin_table, second_half * cos_table + first_half * sin_table], axis=-1)
    return rotated.astype(jnp.bfloat16)


def project_token(tokens, positions, w_q, w_k, w_v, attn_norm, q_norm, k_norm):
    seq_count = tokens.shape[0]
    head_dim = q_norm.shape[0]
    hidden = rms_scale(tokens.astype(jnp.float32), attn_norm).astype(jnp.bfloat16)
    q_proj = jnp.dot(hidden, w_q, preferred_element_type=jnp.float32).astype(jnp.bfloat16).reshape(seq_count, -1, head_dim)
    k_proj = jnp.dot(hidden, w_k, preferred_element_type=jnp.float32).astype(jnp.bfloat16).reshape(seq_count, -1, head_dim)
    v_new = jnp.dot(hidden, w_v, preferred_element_type=jnp.float32).astype(jnp.bfloat16).reshape(seq_count, -1, head_dim)
    cos_table, sin_table = rope_table(positions, head_dim)
    return norm_rope(q_proj, q_norm, cos_table, sin_table), norm_rope(k_proj, k_norm, cos_table, sin_table), v_new


def local_attention(q_rot, k_rot, v_new, positions, k_loc, v_loc, shard_start):
    seq_count, slot_count, kv_heads, head_dim = k_loc.shape
    q_per_kv = q_rot.shape[1] // kv_heads
    score_scale = head_dim ** -0.5
    slot_ids = shard_start + jnp.arange(slot_count)
    write_mask = (slot_ids[None, :] == positions[:, None])[:, :, None, None]
    k_upd = jnp.where(write_mask, k_rot[:, None], k_loc)
    v_upd = jnp.where(write_mask, v_new[:, None], v_loc)
    q_grp = q_rot.reshape(seq_count, kv_heads, q_per_kv, head_dim)
    scores = jnp.einsum('bkgd,btkd->bkgt', q_grp, k_upd, preferred_element_type=jnp.float32) * score_scale
    live_mask = (slot_ids[None, :] <= positions[:, None])[:, None, None, :]
    local_peak = jnp.max(jnp.where(live_mask, scores, NEG_FILL), axis=-1)
    weights = jnp.where(live_mask, jnp.exp(scores - local_peak[..., None]), 0.0)
    local_sum = jnp.sum(weights, axis=-1)
    local_out = jnp.einsum('bkgt,btkd->bkgd', weights.astype(jnp.bfloat16), v_upd, preferred_element_type=jnp.float32)
    return k_upd, v_upd, local_peak, local_sum, local_out


def solution(mesh):
    cache_spec = P('dp', 'sp', None, None)

    def device_step(tokens, positions, k_cache, v_cache, w_q, w_k, w_v, w_o, attn_norm, q_norm, k_norm):
        q_rot, k_rot, v_new = project_token(tokens, positions, w_q, w_k, w_v, attn_norm, q_norm, k_norm)
        head_dim = q_norm.shape[0]
        shard_start = lax.axis_index('sp') * k_cache.shape[1]
        k_upd, v_upd, local_peak, local_sum, local_out = local_attention(q_rot, k_rot, v_new, positions, k_cache, v_cache, shard_start)
        global_peak = lax.pmax(local_peak, 'sp')
        factor = jnp.exp(local_peak - global_peak)
        packed = jnp.concatenate([local_out * factor[..., None], (local_sum * factor)[..., None]], axis=-1)
        summed = lax.psum(packed, 'sp')
        attn_out = (summed[..., :head_dim] / summed[..., head_dim:]).astype(jnp.bfloat16).reshape(tokens.shape[0], -1)
        block_out = (tokens.astype(jnp.float32) + jnp.dot(attn_out, w_o, preferred_element_type=jnp.float32)).astype(jnp.bfloat16)
        return block_out, k_upd, v_upd, jnp.stack([k_rot, v_new], axis=1)

    return jax.shard_map(device_step, mesh=mesh, in_specs=(P('dp', None), P('dp'), cache_spec, cache_spec, P(), P(), P(), P(), P(), P(), P()), out_specs=(P('dp', None), cache_spec, cache_spec, P('dp', None, None, None)), check_vma=False)
```

profile of v0, /device:TPU:1, one launch (start us, length us, event | category | flops | bytes accessed | tf_op | source)
XLA Modules:
  0.0 288.3 jit_solution(9992883581225042052)
XLA Ops:
  7.2 0.7 convert_element_type.66
  7.9 0.7 convert_element_type.71
  8.6 0.7 convert_element_type.67
  9.2 1.1 fusion.19
  10.4 0.7 convert_element_type.61
  11.1 0.7 broadcast_compare_fusion.1
  11.8 3.8 %fusion.15 = bf16[8,8,8,128]{3,1,2,0:T(8,128)(2,1)S(1)} fusion(bf16[2560,1024]{1,0:T(8,128)(2,1)} %param.17, bf16[64,2560]{1,0:T(8,128)(2,1)} %param.11, f32[2560]{0:T(1024)S(1)} %convert_element_type.61, f32[64]{0:T(128)S(1)} %add_rsqrt_fusion.2), kind=kOutput, calls=%fused_computation.18 | convolution fusion | flops 336265216 | bytes 5712128 | tf_op jit(solution)/shard_map/dot_general | solution.py:36
  15.7 0.4 copy-done.1
  16.1 1.1 fusion.14
  17.5 9.0 %fusion.6 = f32[8,8,32,128]{3,1,2,0:T(8,128)S(1)} fusion(bf16[2560,4096]{1,0:T(8,128)(2,1)} %param.15, bf16[64,2560]{1,0:T(8,128)(2,1)S(1)} %copy-done, f32[2560]{0:T(1024)S(1)} %convert_element_type.61, f32[64]{0:T(128)S(1)} %add_rsqrt_fusion.2), kind=kOutput, calls=%fused_computation.11 | convolution fusion | flops 1343356928 | bytes 22358272 | tf_op jit(solution)/shard_map/dot_general | solution.py:34
  26.5 0.2 copy.58
  26.7 0.3 multiply_reduce_fusion
  27.1 0.2 multiply_cosine_fusion
  27.4 0.3 multiply_multiply_fusion
  27.9 0.5 subtract_convert_fusion
  28.6 0.8 copy-done.3
  29.3 0.6 copy-done.4
  30.0 2.6 broadcast_select_fusion
  32.6 1.6 select_reduce_fusion
  34.2 70.3 %pmax.7 = f32[64,8,4]{2,1,0:T(8,128)S(1)} all-reduce(f32[64,8,4]{2,1,0:T(8,128)S(1)} %get-tuple-element.16), channel_id=1, replica_groups=mesh['dp'=1,'sp'=128] {'sp'}, use_global_device_ids=true, to_apply=%region_4.5 | all-reduce | flops 2048 | bytes 16384 | tf_op jit(solution)/shard_map/pmax | solution.py:67
  104.5 1.3 fusion.17
  105.9 0.8 multiply_bitcast_fusion
  106.6 3.2 %copy.50 = f32[64,8,4,1]{3,2,1,0:T(4,128)S(1)} copy(f32[64,8,4,1]{2,1,0,3:T(8,128)S(1)} %get-tuple-element.4) | data formatting | bytes 16384 | tf_op jit(solution)/shard_map/broadcast_in_dim | solution.py:69
  109.8 2.6 fusion.10
  112.5 1.9 pad_maximum_fusion
  114.4 0.8 pad_maximum_fusion.1
  115.2 147.8 %all-reduce.2.cloned.1.call-done = f32[64,8,4,129]{3,2,1,0:T(4,128)} async-done(((f32[64,8,4,129]{3,2,1,0:T(4,128)}), f32[64,8,4,129]{3,2,1,0:T(4,128)}) %all-reduce.2.cloned.1.call-update) | async-done | bytes 1056784 | tf_op jit(solution)/shard_map/psum | solution.py:70
  263.0 1.2 slice-done
  264.3 3.8 %copy.57 = f32[64,8,4,1]{2,1,0,3:T(8,128)} copy(f32[64,8,4,1]{3,2,1,0:T(4,128)S(1)} %slice-done) | data formatting | bytes 16384 | tf_op jit(solution)/shard_map/div | solution.py:71
  268.0 1.6 fusion.16
  269.7 0.4 reshape.191
  270.1 11.4 %fusion.1 = bf16[64,2560]{1,0:T(8,128)(2,1)} fusion(bf16[64,4096]{1,0:T(8,128)(2,1)S(1)} %reshape.191, bf16[4096,2560]{1,0:T(8,128)(2,1)} %param.18, bf16[64,2560]{1,0:T(8,128)(2,1)S(1)} %copy-done), kind=kOutput, calls=%fused_computation.3 | convolution fusion | flops 1342668800 | bytes 22151168 | tf_op jit(solution)/shard_map/dot_general | solution.py:72
  (25 shorter events, 0.9 us)
Async XLA Ops:
  7.2 255.9 %all-reduce.2.cloned.1.call-start = ((), (), s32[]{:S(2)}) async-start(), calls=%async_computation | async-start | bytes 4194304 | tf_op jit(solution)/shard_map/psum | solution.py:70
  11.8 3.9 %copy-start = (bf16[64,2560]{1,0:T(8,128)(2,1)S(1)}, bf16[64,2560]{1,0:T(8,128)(2,1)}, u32[]{:S(2)}) copy-start(bf16[64,2560]{1,0:T(8,128)(2,1)} %param.11) | copy-start | bytes 983044
  11.8 4.2 %copy-start.1 = (bf16[2560,1024]{1,0:T(8,128)(2,1)S(1)}, bf16[2560,1024]{1,0:T(8,128)(2,1)}, u32[]{:S(2)}) copy-start(bf16[2560,1024]{1,0:T(8,128)(2,1)} %param.16) | copy-start | bytes 15728644
  27.8 1.6 copy-start.3
  27.8 2.2 copy-start.4
  32.6 1.6 copy-start.5
  263.0 1.2 slice-start
  263.0 5.0 %copy-start.2 = (f32[64,8,4,129]{3,2,1,0:T(4,128)S(1)}, f32[64,8,4,129]{3,2,1,0:T(4,128)}, u32[]{:S(2)}) copy-start(f32[64,8,4,129]{3,2,1,0:T(4,128)} %all-reduce.2.cloned.1.call-done) | copy-start | bytes 3170308
Sparse Core Ops, SparseCore 0:
  114.5 148.4 all-reduce.1
where the time goes:
time: 289 us; the launch traced here: 288 us
  waiting for transfers between devices  148 us (51%)
  blocking collectives  70.3 us (24%)
  matrix products  29.5 us (10%)
  other arithmetic  15.6 us (5%)
  between operations  14.3 us (5%)
  local copies, waits for them, and re-layouts  10.8 us (4%)
    psum x1, waiting for transfers between devices, device_step(): summed = lax.psum(packed, 'sp')  148 us
    pmax x1, blocking collectives, device_step(): global_peak = lax.pmax(local_peak, 'sp')  70.3 us
    dot_general x1, matrix products, device_step(): jnp.dot(attn_out, w_o, preferred_element_type=jnp.float32)  11.4 us
    dot_general x1, matrix products, project_token(): jnp.dot(hidden, w_q, preferred_element_type=jnp.float32)  8.99 us
  transfers between devices with their start and end apart: 1, of which 1 were waited for; matrix products, arithmetic and copies ran while one was open for 0% of the time, Pallas kernels for 0%

commit v1 on v0

v1 whole, which is shorter than its diff:
```python
import functools

import jax
import jax.numpy as jnp
import numpy as np
from jax import lax
from jax.experimental import pallas as pl
from jax.experimental.pallas import tpu as pltpu
from jax.sharding import PartitionSpec as P

NORM_EPS = 1e-6
ROPE_THETA = 1000000.0
NEG_FILL = -1e30
SEQS, DIM, HEADS, KV_HEADS, HEAD_DIM, SLOTS = 64, 2560, 32, 8, 128, 16
HALF = HEADS // 2
CHIPS = 64
SCALE = HEAD_DIM ** -0.5
F32, BF16 = jnp.float32, jnp.bfloat16
MESH = pl.DeviceIdType.MESH
DEPTH = 4


def rms(values, gain):
    return values * lax.rsqrt(jnp.mean(values * values, axis=-1, keepdims=True) + NORM_EPS) * gain


def iota(shape, axis):
    return lax.broadcasted_iota(jnp.int32, shape, axis)


def pick(row, lane):
    spread = jnp.broadcast_to(row, (HALF, HEAD_DIM))
    return jnp.sum(jnp.where(lane, spread, 0.0), axis=-1, keepdims=True)


def step_kernel(pos_ref, tok_ref, an_ref, qn_ref, kn_ref, freq_ref, wq_hbm, wk_hbm, wv_hbm, wo_hbm, kc_hbm, vc_hbm,
                out_ref, kv_hbm,
                hid, cosr, sinr, wbuf, wobuf, kbuf, vbuf, gbuf, obuf, oin, st, stin, osend, stsend, rbuf, rst,
                lhs, ypart, yin, ysend, ybuf,
                wsem, wosem, csem, kvsem, gsend, grecv, dsend, drecv, dssend, dsrecv,
                ssend, srecv, tsend, trecv, ysem, bsend, brecv, fsend, frecv):
    me = lax.axis_index("sp")
    chip, core = me // 2, me % 2
    zed = chip // 16
    mate = chip * 2 + (1 - core)
    start = me * SLOTS

    def dev(index):
        return (lax.axis_index("dp"), index)

    barrier = pltpu.get_barrier_semaphore()
    pl.semaphore_signal(barrier, inc=1, device_id=dev(mate), device_id_type=MESH)

    @pl.loop(1, CHIPS)
    def _(off):
        pl.semaphore_signal(barrier, inc=1, device_id=dev(lax.rem(chip + off, CHIPS) * 2 + core), device_id_type=MESH)

    def wcopy(src, col, tile):
        return pltpu.make_async_copy(src.at[:, pl.ds(pl.multiple_of(col, 256), 256)], wbuf.at[tile], wsem.at[tile])

    def kcopy(t):
        return wcopy(wk_hbm, core * 512 + t * 256, t)

    def vcopy(t):
        return wcopy(wv_hbm, core * 512 + t * 256, 2 + t)

    def qcopy(t):
        return wcopy(wq_hbm, core * 2048 + t * 256, 4 + t)

    for t in range(2):
        kcopy(t).start()
    for t in range(2):
        vcopy(t).start()

    tok = tok_ref[...].astype(F32)
    hid[...] = rms(tok, an_ref[...].astype(F32)).astype(BF16)
    row8 = iota((SEQS, HEAD_DIM), 0)
    posv = jnp.zeros((SEQS, HEAD_DIM), jnp.int32)
    for s in range(SEQS):
        posv = jnp.where(row8 == s, pos_ref[s], posv)
    angle = posv.astype(F32) * freq_ref[...]
    cosr[...] = jnp.cos(angle)
    sinr[...] = jnp.where(iota((SEQS, HEAD_DIM), 1) < HEAD_DIM // 2, -1.0, 1.0) * jnp.sin(angle)

    def project(tile):
        return jnp.dot(hid[...], wbuf[tile], preferred_element_type=F32).astype(BF16).astype(F32)

    def rope(head, gain):
        normed = rms(head, gain)
        turned = normed * cosr[...] + pltpu.roll(normed, HEAD_DIM // 2, 1) * sinr[...]
        return turned.astype(BF16).astype(F32)

    for t in range(2):
        kcopy(t).wait()
        qcopy(t).start()
        res = project(t)
        for h in range(2):
            gbuf[4 + core, :, 2 * t + h, :] = rope(res[:, h * 128:(h + 1) * 128], kn_ref[...].astype(F32))
    for t in range(2):
        vcopy(t).wait()
        qcopy(2 + t).start()
        res = project(2 + t)
        for h in range(2):
            gbuf[4 + core, :, 4 + 2 * t + h, :] = res[:, h * 128:(h + 1) * 128]

    pl.semaphore_wait(barrier, CHIPS)

    def gcopy(group, slot):
        return pltpu.make_async_remote_copy(src_ref=gbuf.at[group], dst_ref=gbuf.at[group], send_sem=gsend.at[slot],
                                            recv_sem=grecv.at[slot], device_id=dev(mate), device_id_type=MESH)

    gcopy(4 + core, 2).start()

    def kvload(i):
        rows = pl.ds(i * 16, 16)
        return (pltpu.make_async_copy(kc_hbm.at[rows], kbuf.at[rows], csem.at[0, i]),
                pltpu.make_async_copy(vc_hbm.at[rows], vbuf.at[rows], csem.at[1, i]))

    for g in range(2):
        for t4 in range(4):
            t = g * 4 + t4
            qcopy(t).wait()
            if t + DEPTH < 8:
                qcopy(t + DEPTH).start()
            else:
                for c in kvload(t - 4):
                    c.start()
            res = project(4 + t)
            for h in range(2):
                gbuf[2 * core + g, :, 2 * t4 + h, :] = rope(res[:, h * 128:(h + 1) * 128], qn_ref[...].astype(F32))
        gcopy(2 * core + g, g).start()

    wocopy = pltpu.make_async_copy(wo_hbm.at[pl.ds(pl.multiple_of(core * 2048, 2048), 2048)], wobuf, wosem.at[0])
    wocopy.start()
    for slot in range(3):
        gcopy(4 + core if slot == 2 else 2 * core + slot, slot).wait()
    kvout = pltpu.make_async_copy(gbuf.at[pl.ds(4, 2)], kv_hbm, kvsem.at[0])
    kvout.start()
    for i in range(4):
        for c in kvload(i):
            c.wait()

    def block_of(i):
        return lax.rem(zed + 2 + 3 * (i // 2), 4) * 2 + lax.rem(i, 2)

    row32, col32 = iota((HEADS, HEAD_DIM), 0), iota((HEADS, HEAD_DIM), 1)
    same_head = (col32 % KV_HEADS) == (row32 // 4)
    slot_of = col32 // KV_HEADS + start
    row16, lane16 = iota((HALF, HEAD_DIM), 0), iota((HALF, HEAD_DIM), 1)

    def dcopies(blk, i):
        rows = pl.ds(blk * 8, 8)
        return (pltpu.make_async_remote_copy(src_ref=obuf.at[1 - core, rows], dst_ref=oin.at[rows], send_sem=dsend.at[i],
                                             recv_sem=drecv.at[i], device_id=dev(mate), device_id_type=MESH),
                pltpu.make_async_remote_copy(src_ref=st.at[1 - core, blk], dst_ref=stin.at[blk], send_sem=dssend.at[i],
                                             recv_sem=dsrecv.at[i], device_id=dev(mate), device_id_type=MESH))

    def attend(i):
        blk = block_of(i)
        acc = [[jnp.zeros((HALF, HEAD_DIM), F32) for _ in range(2)] for _ in range(2)]
        for s8 in range(8):
            s = blk * 8 + s8
            q = jnp.concatenate([gbuf[g, s] for g in range(4)], axis=0).astype(BF16)
            scores = lax.dot_general(q, kbuf[s], (((1,), (1,)), ((), ())), preferred_element_type=F32) * SCALE
            live = same_head & (slot_of < pos_ref[s])
            scores = jnp.where(live, scores, NEG_FILL)
            peak = jnp.max(scores, axis=-1, keepdims=True)
            weights = jnp.where(live, jnp.exp(scores - peak), 0.0)
            total = jnp.sum(weights, axis=-1, keepdims=True)
            mixed = jnp.dot(weights.astype(BF16), vbuf[s], preferred_element_type=F32)
            here = lane16 == s8 * HALF + row16
            for half in range(2):
                cut = slice(half * HALF, (half + 1) * HALF)
                obuf[half, s] = mixed[cut]
                acc[half][0] += jnp.where(here, peak[cut], 0.0)
                acc[half][1] += jnp.where(here, total[cut], 0.0)
        for half in range(2):
            for k in range(2):
                st[half, blk, pl.ds(k, 1), :] = jnp.sum(acc[half][k], axis=0, keepdims=True)
        for c in dcopies(blk, i):
            c.start()

    def scatter(blk, s):
        o = pltpu.make_async_remote_copy(src_ref=osend.at[s], dst_ref=rbuf.at[chip], send_sem=ssend.at[0], recv_sem=srecv.at[0],
                                         device_id=dev(s * 2 + core), device_id_type=MESH)
        t = pltpu.make_async_remote_copy(src_ref=stsend.at[blk], dst_ref=rst.at[chip], send_sem=tsend.at[0], recv_sem=trecv.at[0],
                                         device_id=dev(s * 2 + core), device_id_type=MESH)
        return o, t

    def merge(i):
        blk = block_of(i)
        for c in dcopies(blk, i):
            c.wait()
        m0, l0 = st[core, blk, pl.ds(0, 1), :], st[core, blk, pl.ds(1, 1), :]
        m1, l1 = stin[blk, pl.ds(0, 1), :], stin[blk, pl.ds(1, 1), :]
        top = jnp.maximum(m0, m1)
        f0, f1 = jnp.exp(m0 - top), jnp.exp(m1 - top)
        stsend[blk, pl.ds(0, 1), :] = top
        stsend[blk, pl.ds(1, 1), :] = l0 * f0 + l1 * f1
        for s8 in range(8):
            s = blk * 8 + s8
            here = lane16 == s8 * HALF + row16
            osend[s] = obuf[core, s] * pick(f0, here) + oin[s] * pick(f1, here)

        @pl.loop(0, 8)
        def _(s8):
            s = blk * 8 + s8

            @pl.when(s != chip)
            def _():
                for c in scatter(blk, s):
                    c.start()

            @pl.when(s == chip)
            def _():
                pltpu.make_async_copy(osend.at[s], rbuf.at[chip], srecv.at[0]).start()
                pltpu.make_async_copy(stsend.at[blk], rst.at[chip], trecv.at[0]).start()

    LAG = 3

    @pl.loop(0, 8 + LAG)
    def _(i):
        @pl.when(i < 8)
        def _():
            attend(i)

        @pl.when(i >= LAG)
        def _():
            merge(i - LAG)

    def all_of(src, dst, send, recv):
        return pltpu.make_async_remote_copy(src_ref=src, dst_ref=dst, send_sem=send, recv_sem=recv, device_id=dev(mate),
                                            device_id_type=MESH)

    all_of(rst, rst, tsend.at[0], trecv.at[0]).wait_recv()
    all_of(rbuf, rbuf, ssend.at[0], srecv.at[0]).wait_recv()

    here = lane16 == lax.rem(chip, 8) * HALF + row16
    tops = rst[:, 0, :]
    top = jnp.max(tops, axis=0, keepdims=True)
    facs = jnp.exp(tops - top)
    total = pick(jnp.sum(rst[:, 1, :] * facs, axis=0, keepdims=True), here)
    acc = jnp.zeros((HALF, HEAD_DIM), F32)
    for c in range(CHIPS):
        acc += rbuf[c] * pick(facs[c:c + 1], here)
    q_own = jnp.concatenate([gbuf[2 * core, chip], gbuf[2 * core + 1, chip]], axis=0)
    kv_own = gbuf[4 + core, chip]
    k_own = jnp.concatenate([jnp.broadcast_to(kv_own[i:i + 1], (4, HEAD_DIM)) for i in range(4)], axis=0)
    v_own = jnp.concatenate([jnp.broadcast_to(kv_own[4 + i:5 + i], (4, HEAD_DIM)) for i in range(4)], axis=0)
    s_own = jnp.sum(q_own * k_own, axis=-1, keepdims=True) * SCALE
    top = pick(top, here)
    peak = jnp.maximum(top, s_own)
    f_old, f_new = jnp.exp(top - peak), jnp.exp(s_own - peak)
    attn = (acc * f_old + v_own * f_new) / (total * f_old + f_new)
    for h in range(HALF):
        lhs[:, h * 128:(h + 1) * 128] = jnp.where(row16 == h, attn, 0.0).astype(BF16)

    wocopy.wait()

    def out_cols(half, slot):
        for n in range(5):
            cols = pl.ds(pl.multiple_of(half * 1280 + n * 256, 256), 256)
            res = jnp.dot(lhs[...], wobuf[:, cols], preferred_element_type=F32)
            res = jnp.sum(res, axis=0, keepdims=True)
            for k in range(2):
                ypart[slot, pl.ds(2 * n + k, 1), :] = res[:, k * 128:(k + 1) * 128]

    out_cols(1 - core, 0)
    ycopy = pltpu.make_async_remote_copy(src_ref=ypart.at[0], dst_ref=yin, send_sem=ysem.at[0], recv_sem=ysem.at[1],
                                         device_id=dev(mate), device_id_type=MESH)
    ycopy.start()
    out_cols(core, 1)
    ycopy.wait()
    ysend[...] = ypart[1] + yin[...]

    def bcopy(s, group):
        return pltpu.make_async_remote_copy(src_ref=ysend, dst_ref=ybuf.at[core, chip], send_sem=bsend.at[0],
                                            recv_sem=brecv.at[group], device_id=dev(s * 2 + core), device_id_type=MESH)

    @pl.loop(0, CHIPS)
    def _(k):
        s = lax.rem(chip + 32 + k, CHIPS)
        group = lax.rem(zed - s // 16 + 4, 4)

        @pl.when(s != chip)
        def _():
            bcopy(s, group).start()

        @pl.when(s == chip)
        def _():
            pltpu.make_async_copy(ysend, ybuf.at[core, chip], brecv.at[0]).start()

    def slab(half, group):
        return ybuf.at[half, pl.ds(lax.rem(zed + group, 4) * 16, 16)]

    def fcopy(half, group):
        ref = slab(half, group)
        return pltpu.make_async_remote_copy(src_ref=ref, dst_ref=ref, send_sem=fsend.at[group], recv_sem=frecv.at[group],
                                            device_id=dev(mate), device_id_type=MESH)

    for group in (0, 1, 3, 2):
        ref = slab(core, group)
        all_of(ref, ref, bsend.at[0], brecv.at[group]).wait_recv()
        fcopy(core, group).start()
    for group in (0, 1, 3, 2):
        fcopy(1 - core, group).wait_recv()

    for half in range(2):
        for k in range(10):
            cols = slice(half * 1280 + k * 128, half * 1280 + (k + 1) * 128)
            out_ref[:, cols] = (tok_ref[:, cols].astype(F32) + ybuf[half, :, k, :]).astype(BF16)

    for group in range(4):
        fcopy(core, group).wait_send()
    all_of(rst.at[pl.ds(0, CHIPS - 1)], rst.at[pl.ds(0, CHIPS - 1)], tsend.at[0], trecv.at[0]).wait_send()
    all_of(rbuf.at[pl.ds(0, CHIPS - 1)], rbuf.at[pl.ds(0, CHIPS - 1)], ssend.at[0], srecv.at[0]).wait_send()
    rest = ybuf.at[0, pl.ds(0, CHIPS - 1)]
    all_of(rest, rest, bsend.at[0], brecv.at[0]).wait_send()
    kvout.wait()


def step_call(*args):
    dma = pltpu.SemaphoreType.DMA
    vmem = pltpu.VMEM
    blk = pl.BlockSpec(memory_space=pltpu.VMEM)
    hbm = pl.BlockSpec(memory_space=pl.ANY)
    return pl.pallas_call(
        step_kernel,
        name="decode_step",
        out_shape=(jax.ShapeDtypeStruct((SEQS, DIM), BF16), jax.ShapeDtypeStruct((2, SEQS, 8, HEAD_DIM), F32)),
        in_specs=[pl.BlockSpec(memory_space=pltpu.SMEM)] + [blk] * 5 + [hbm] * 6,
        out_specs=(blk, hbm),
        scratch_shapes=[
            vmem((SEQS, DIM), BF16), vmem((SEQS, HEAD_DIM), F32), vmem((SEQS, HEAD_DIM), F32),
            vmem((12, DIM, 256), BF16), vmem((2048, DIM), BF16),
            vmem((SEQS, 128, HEAD_DIM), BF16), vmem((SEQS, 128, HEAD_DIM), BF16),
            vmem((6, SEQS, 8, HEAD_DIM), F32),
            vmem((2, SEQS, HALF, HEAD_DIM), F32), vmem((SEQS, HALF, HEAD_DIM), F32),
            vmem((2, 8, 2, HEAD_DIM), F32), vmem((8, 2, HEAD_DIM), F32),
            vmem((SEQS, HALF, HEAD_DIM), F32), vmem((8, 2, HEAD_DIM), F32),
            vmem((CHIPS, HALF, HEAD_DIM), F32), vmem((CHIPS, 2, HEAD_DIM), F32),
            vmem((HALF, 2048), BF16), vmem((2, 10, HEAD_DIM), F32), vmem((10, HEAD_DIM), F32), vmem((10, HEAD_DIM), F32),
            vmem((2, CHIPS, 10, HEAD_DIM), F32),
            dma((12,)), dma((1,)), dma((2, 4)), dma((1,)), dma((3,)), dma((3,)), dma((8,)), dma((8,)), dma((8,)), dma((8,)),
            dma((1,)), dma((1,)), dma((1,)), dma((1,)), dma((2,)), dma((1,)), dma((4,)), dma((4,)), dma((4,)),
        ],
        compiler_params=pltpu.CompilerParams(collective_id=0, has_side_effects=True, vmem_limit_bytes=60 * 2 ** 20),
    )(*args)


CHUNKS = 8


def cache_kernel(pos_ref, kv_ref, kc_hbm, vc_hbm, ko_hbm, vo_hbm, new_ref, kbuf, vbuf, isem, osem):
    start = lax.axis_index("sp") * SLOTS
    per = SEQS // CHUNKS

    def copies(i, out):
        rows = pl.ds(i * per, per)
        if out:
            return (pltpu.make_async_copy(kbuf.at[rows], ko_hbm.at[rows], osem.at[0, i]),
                    pltpu.make_async_copy(vbuf.at[rows], vo_hbm.at[rows], osem.at[1, i]))
        return (pltpu.make_async_copy(kc_hbm.at[rows], kbuf.at[rows], isem.at[0, i]),
                pltpu.make_async_copy(vc_hbm.at[rows], vbuf.at[rows], isem.at[1, i]))

    for i in range(CHUNKS):
        for c in copies(i, False):
            c.start()
    low = iota((SEQS, 8, HEAD_DIM), 1) < 4
    first, second = kv_ref[0], kv_ref[1]
    new_ref[:, 0] = jnp.where(low, first, pltpu.roll(second, 4, 1)).astype(BF16)
    new_ref[:, 1] = jnp.where(low, pltpu.roll(first, 4, 1), second).astype(BF16)
    for i in range(CHUNKS):
        for c in copies(i, False):
            c.wait()

        @pl.loop(i * per, (i + 1) * per)
        def _(s):
            slot = pos_ref[s] - start

            @pl.when((slot >= 0) & (slot < SLOTS))
            def _():
                kbuf[s, slot] = new_ref[s, 0]
                vbuf[s, slot] = new_ref[s, 1]

        for c in copies(i, True):
            c.start()
    for i in range(CHUNKS):
        for c in copies(i, True):
            c.wait()


def cache_call(*args):
    hbm = pl.BlockSpec(memory_space=pl.ANY)
    blk = pl.BlockSpec(memory_space=pltpu.VMEM)
    shape = (SEQS, SLOTS, KV_HEADS, HEAD_DIM)
    dma = pltpu.SemaphoreType.DMA
    return pl.pallas_call(
        cache_kernel,
        name="cache_write",
        out_shape=(jax.ShapeDtypeStruct(shape, BF16), jax.ShapeDtypeStruct(shape, BF16),
                   jax.ShapeDtypeStruct((SEQS, 2, KV_HEADS, HEAD_DIM), BF16)),
        in_specs=[pl.BlockSpec(memory_space=pltpu.SMEM), blk, hbm, hbm],
        out_specs=(hbm, hbm, blk),
        scratch_shapes=[pltpu.VMEM(shape, BF16), pltpu.VMEM(shape, BF16), dma((2, CHUNKS)), dma((2, CHUNKS))],
    )(*args)


def solution(mesh):
    cache_spec = P('dp', 'sp', None, None)

    def device_step(tokens, positions, k_cache, v_cache, w_q, w_k, w_v, w_o, attn_norm, q_norm, k_norm):
        inv = np.float32(ROPE_THETA) ** (-np.arange(HEAD_DIM // 2, dtype=np.float32) * np.float32(2.0) / np.float32(HEAD_DIM))
        freq = jnp.asarray(np.concatenate([inv, inv])[None, :].astype(np.float32))
        flat = (SEQS, SLOTS * KV_HEADS, HEAD_DIM)
        block_out, kv = step_call(positions, tokens, attn_norm[None, :], q_norm[None, :], k_norm[None, :], freq, w_q, w_k, w_v,
                                  w_o, k_cache.reshape(flat), v_cache.reshape(flat))
        k_out, v_out, new_kv = cache_call(positions, kv, k_cache, v_cache)
        return block_out, k_out, v_out, new_kv

    return jax.shard_map(device_step, mesh=mesh, in_specs=(P('dp', None), P('dp'), cache_spec, cache_spec, P(), P(), P(), P(), P(), P(), P()), out_specs=(P('dp', None), cache_spec, cache_spec, P('dp', None, None, None)), check_vma=False)
```

time: 289 us -> 66.1 us (0.23)
  waiting for transfers between devices: 148 us -> 0 us
  blocking collectives: 70.3 us -> 0 us
  Pallas kernels: 0 us -> 62.2 us
  matrix products: 29.5 us -> 0 us
  other arithmetic: 15.6 us -> 0 us
  between operations: 14.3 us -> 0.65 us
  local copies, waits for them, and re-layouts: 10.8 us -> 3.02 us
    psum x1 -> x0, waiting for transfers between devices: 148 us -> none  [device_step(): summed = lax.psum(packed, 'sp')]
    pmax x1 -> x0, blocking collectives: 70.3 us -> none  [device_step(): global_peak = lax.pmax(local_peak, 'sp')]
    pallas_call x0 -> x2, Pallas kernels: none -> 62.2 us  [the longest x1 56.7 us: step_call(): pl.pallas_call(step_kernel, name='decode_step', out_shape=(jax.ShapeDtype...]
    dot_general x6 -> x0, matrix products: 29.5 us -> none  [the longest x1 11.4 us: device_step(): jnp.dot(attn_out, w_o, preferred_element_type=jnp.float32)]
    convert_element_type x5 -> x0, other arithmetic: 4.31 us -> none  [the longest x3 2.02 us: rms_scale(): gain.astype(jnp.float32)]
    div x1 -> x0, local copies, waits for them, and re-layouts: 3.78 us -> none  [device_step(): summed[..., :head_dim] / summed[..., head_dim:]]
    reduce_sum x4 -> x0, other arithmetic: 2.96 us -> none  [the longest x3 1.62 us: rms_scale(): jnp.mean(values * values, axis=-1, keepdims=True) + NORM_EPS]
  transfers between devices with their start and end apart: 1 -> 0, of which waited for: 1 -> 0; matrix products, arithmetic and copies ran while one was open for 0% -> 0% of each run, Pallas kernels for 0% -> 0%
where the time goes in v1:
time: 66.1 us; the launch traced here: 65.9 us
  Pallas kernels  62.2 us (94%)
  local copies, waits for them, and re-layouts  3.02 us (5%)
    pallas_call x1, Pallas kernels, step_call(): pl.pallas_call(step_kernel, name='decode_step', out_shape=(jax.ShapeDtype...  56.7 us
    pallas_call x1, Pallas kernels, cache_call(): pl.pallas_call(cache_kernel, name='cache_write', out_shape=(jax.ShapeDtyp...  5.48 us
    unnamed x1, local copies, waits for them, and re-layouts  1.72 us

profile of v1, /device:TPU:1, one launch (start us, length us, event | category | flops | bytes accessed | tf_op | source)
XLA Modules:
  0.0 65.9 jit_solution(247293714998651915)
XLA Ops:
  0.6 1.3 %broadcast_in_dim.9.an_ref = bf16[1,2560]{1,0:T(2,128)(2,1)} reshape(bf16[2560]{0:T(1024)(128)(2,1)} %param.20) | data formatting | bytes 10240 | tf_op jit(solution)/shard_map/broadcast_in_dim | solution.py:416
  1.9 56.7 %decode_step.1 = (bf16[64,2560]{1,0:T(8,128)(2,1)}, f32[2,64,8,128]{3,2,1,0:T(8,128)}) custom-call(s32[64]{0:T(128)} %pos_ref.3, bf16[64,2560]{1,0:T(8,128)(2,1)} %tok_ref.1, bf16[1,2560]{1,0:T(2,128)(2,1)} %broadcast_in_dim.9.an_ref, bf16[1,128]{1,0:T(2,128)(2,1)} %bitcast.6, bf16[1,128]{1,0:T(2,128)(2,1)} %bitcast.7, f32[1,128]{1,0:T(1,128)} %constant.2.clone.freq_ref, ...), custom_call_target="tpu_custom_call" | custom-call | tf_op jit(solution)/shard_map/decode_step/pallas_call | solution.py:327
  58.6 5.5 %cache_write.1 = (bf16[64,16,8,128]{3,2,1,0:T(8,128)(2,1)}, bf16[64,16,8,128]{3,2,1,0:T(8,128)(2,1)}, bf16[64,2,8,128]{3,2,1,0:T(8,128)(2,1)}) custom-call(s32[64]{0:T(128)} %pos_ref.3, f32[2,64,8,128]{3,2,1,0:T(8,128)} %get-tuple-element.10.kv_ref, bf16[64,16,8,128]{3,2,1,0:T(8,128)(2,1)} %kc_hbm.1, bf16[64,16,8,128]{3,2,1,0:T(8,128)(2,1)} %vc_hbm.1), custom_call_target="tpu_custom_call" | custom-call | tf_op jit(solution)/shard_map/cache_write/pallas_call | solution.py:398
  64.1 1.7 %copy.17 = bf16[64,2560]{1,0:T(8,128)(2,1)} copy(bf16[64,2560]{1,0:T(8,128)(2,1)} %get-tuple-element.18) | data formatting | bytes 655360

commit v2 on v1

v2 whole, which is shorter than its diff:
```python
import functools

import jax
import jax.numpy as jnp
import numpy as np
from jax import lax
from jax.experimental import pallas as pl
from jax.experimental.pallas import tpu as pltpu
from jax.sharding import PartitionSpec as P

NORM_EPS = 1e-6
ROPE_THETA = 1000000.0
NEG_FILL = -1e30
SEQS, DIM, HEADS, KV_HEADS, HEAD_DIM, SLOTS = 64, 2560, 32, 8, 128, 16
HALF = HEADS // 2
CHIPS = 64
SCALE = HEAD_DIM ** -0.5
F32, BF16 = jnp.float32, jnp.bfloat16
MESH = pl.DeviceIdType.MESH
DEPTH = 3
LAG = 5


def rms(values, gain):
    return values * lax.rsqrt(jnp.mean(values * values, axis=-1, keepdims=True) + NORM_EPS) * gain


def iota(shape, axis):
    return lax.broadcasted_iota(jnp.int32, shape, axis)


def pick(row, lane):
    spread = jnp.broadcast_to(row, (HALF, HEAD_DIM))
    return jnp.sum(jnp.where(lane, spread, 0.0), axis=-1, keepdims=True)


def step_kernel(pos_ref, tok_hbm, an_hbm, qn_hbm, kn_hbm, freq_hbm, wq_hbm, wk_hbm, wv_hbm, wo_hbm, kc_hbm, vc_hbm,
                out_hbm, kv_hbm,
                tok_ref, an_ref, qn_ref, kn_ref, freq_ref, isem, outsem, hid, cosr, sinr, wbuf, wobuf, kbuf, vbuf, gbuf, wts, obuf, oin, st, stin, fac, osend, stsend, rbuf, rst, out_ref,
                lhs, ypart, yin, ysend, ybuf,
                wsem, wosem, csem, kvsem, gsend, grecv, dsend, drecv, dssend, dsrecv,
                ssend, srecv, tsend, trecv, ysem, bsend, brecv, fsend, frecv):
    me = lax.axis_index("sp")
    chip, core = me // 2, me % 2
    zed = chip // 16
    mate = chip * 2 + (1 - core)
    start = me * SLOTS

    def dev(index):
        return (lax.axis_index("dp"), index)

    barrier = pltpu.get_barrier_semaphore()
    pl.semaphore_signal(barrier, inc=1, device_id=dev(mate), device_id_type=MESH)

    @pl.loop(1, CHIPS)
    def _(off):
        pl.semaphore_signal(barrier, inc=1, device_id=dev(lax.rem(chip + off, CHIPS) * 2 + core), device_id_type=MESH)

    def wcopy(src, col, tile):
        return pltpu.make_async_copy(src.at[:, pl.ds(pl.multiple_of(col, 256), 256)], wbuf.at[tile], wsem.at[tile])

    def tile_copy(t):
        if t < 2:
            return wcopy(wk_hbm, core * 512 + t * 256, t)
        if t < 4:
            return wcopy(wv_hbm, core * 512 + (t - 2) * 256, t)
        return wcopy(wq_hbm, core * 2048 + (t - 4) * 256, t)

    def kvload(i):
        rows = pl.ds(i * 16, 16)
        return (pltpu.make_async_copy(kc_hbm.at[rows], kbuf.at[rows], csem.at[0, i]),
                pltpu.make_async_copy(vc_hbm.at[rows], vbuf.at[rows], csem.at[1, i]))

    def tile_ready(t):
        tile_copy(t).wait()
        if t + DEPTH < 12:
            tile_copy(t + DEPTH).start()
        elif t + DEPTH < 14:
            for c in kvload(2 * (t + DEPTH - 12)) + kvload(2 * (t + DEPTH - 12) + 1):
                c.start()

    inputs = [pltpu.make_async_copy(a, b, isem.at[i]) for i, (a, b) in enumerate(
        [(tok_hbm, tok_ref), (an_hbm, an_ref), (freq_hbm, freq_ref), (kn_hbm, kn_ref), (qn_hbm, qn_ref)])]
    for c in inputs:
        c.start()
    for t in range(DEPTH):
        tile_copy(t).start()
    for c in inputs:
        c.wait()

    tok = tok_ref[...].astype(F32)
    hid[...] = rms(tok, an_ref[...].astype(F32).reshape(1, DIM)).astype(BF16)
    row8 = iota((SEQS, HEAD_DIM), 0)
    posv = jnp.zeros((SEQS, HEAD_DIM), jnp.int32)
    for s in range(SEQS):
        posv = jnp.where(row8 == s, pos_ref[s], posv)
    angle = posv.astype(F32) * freq_ref[...]
    cosr[...] = jnp.cos(angle)
    sinr[...] = jnp.where(iota((SEQS, HEAD_DIM), 1) < HEAD_DIM // 2, -1.0, 1.0) * jnp.sin(angle)

    def project(tile):
        return jnp.dot(hid[...], wbuf[tile], preferred_element_type=F32).astype(BF16).astype(F32)

    def rope(head, gain):
        normed = rms(head, gain)
        turned = normed * cosr[...] + pltpu.roll(normed, HEAD_DIM // 2, 1) * sinr[...]
        return turned.astype(BF16).astype(F32)

    for t in range(4):
        tile_ready(t)
        res = project(t)
        for h in range(2):
            head = res[:, h * 128:(h + 1) * 128]
            gbuf[4 + core, :, 2 * t + h, :] = rope(head, kn_ref[...].astype(F32)) if t < 2 else head

    def gcopy(group, slot):
        return pltpu.make_async_remote_copy(src_ref=gbuf.at[group], dst_ref=gbuf.at[group], send_sem=gsend.at[slot],
                                            recv_sem=grecv.at[slot], device_id=dev(mate), device_id_type=MESH)

    for g in range(2):
        for t4 in range(4):
            t = 4 + g * 4 + t4
            tile_ready(t)
            res = project(t)
            for h in range(2):
                gbuf[2 * core + g, :, 2 * t4 + h, :] = rope(res[:, h * 128:(h + 1) * 128], qn_ref[...].astype(F32))
        if g == 0:
            pl.semaphore_wait(barrier, CHIPS)
            gcopy(4 + core, 2).start()
        gcopy(2 * core + g, g).start()

    wocopy = pltpu.make_async_copy(wo_hbm.at[pl.ds(pl.multiple_of(core * 2048, 2048), 2048)], wobuf, wosem.at[0])
    wocopy.start()
    for slot in range(3):
        gcopy(4 + core if slot == 2 else 2 * core + slot, slot).wait()
    kvout = pltpu.make_async_copy(gbuf.at[pl.ds(4, 2)], kv_hbm, kvsem.at[0])
    kvout.start()
    for i in range(4):
        for c in kvload(i):
            c.wait()

    def block_of(i):
        return lax.rem(zed + 2 + 3 * (i // 2), 4) * 2 + lax.rem(i, 2)

    row32, col32 = iota((HEADS, HEAD_DIM), 0), iota((HEADS, HEAD_DIM), 1)
    same_head = (col32 % KV_HEADS) == (row32 // 4)
    slot_of = col32 // KV_HEADS + start
    row16, lane16 = iota((HALF, HEAD_DIM), 0), iota((HALF, HEAD_DIM), 1)

    def weigh(blk):
        acc = [[jnp.zeros((HALF, HEAD_DIM), F32) for _ in range(2)] for _ in range(2)]
        for s8 in range(8):
            s = blk * 8 + s8
            q = jnp.concatenate([gbuf[g, s] for g in range(4)], axis=0).astype(BF16)
            scores = lax.dot_general(q, kbuf[s], (((1,), (1,)), ((), ())), preferred_element_type=F32) * SCALE
            live = same_head & (slot_of < pos_ref[s])
            scores = jnp.where(live, scores, NEG_FILL)
            peak = jnp.max(scores, axis=-1, keepdims=True)
            weights = jnp.where(live, jnp.exp(scores - peak), 0.0)
            total = jnp.sum(weights, axis=-1, keepdims=True)
            wts[s] = weights.astype(BF16)
            here = lane16 == s8 * HALF + row16
            for half in range(2):
                cut = slice(half * HALF, (half + 1) * HALF)
                acc[half][0] += jnp.where(here, peak[cut], 0.0)
                acc[half][1] += jnp.where(here, total[cut], 0.0)
        for half in range(2):
            for k in range(2):
                st[half, blk, pl.ds(k, 1), :] = jnp.sum(acc[half][k], axis=0, keepdims=True)

    def mix(i):
        blk = block_of(i)
        for s8 in range(8):
            s = blk * 8 + s8
            mixed = jnp.dot(wts[s], vbuf[s], preferred_element_type=F32)
            for half in range(2):
                obuf[half, s] = mixed[half * HALF:(half + 1) * HALF]
        ocopy(i).start()

    def ocopy(i):
        rows = pl.ds(block_of(i) * 8, 8)
        return pltpu.make_async_remote_copy(src_ref=obuf.at[1 - core, rows], dst_ref=oin.at[rows], send_sem=dsend.at[i],
                                            recv_sem=drecv.at[i], device_id=dev(mate), device_id_type=MESH)

    def merge(i):
        blk = block_of(i)
        ocopy(i).wait()
        f0, f1 = fac[0, pl.ds(blk, 1), :], fac[1, pl.ds(blk, 1), :]
        for s8 in range(8):
            s = blk * 8 + s8
            here = lane16 == s8 * HALF + row16
            osend[s] = obuf[core, s] * pick(f0, here) + oin[s] * pick(f1, here)
        for s8 in range(8):
            s = blk * 8 + s8

            @pl.when(s != chip)
            def _():
                pltpu.make_async_remote_copy(src_ref=osend.at[s], dst_ref=rbuf.at[chip], send_sem=ssend.at[0], recv_sem=srecv.at[0],
                                             device_id=dev(s * 2 + core), device_id_type=MESH).start()

    @pl.loop(0, 8)
    def _(blk):
        weigh(blk)

    stcopy = pltpu.make_async_remote_copy(src_ref=st.at[1 - core], dst_ref=stin, send_sem=dssend.at[0], recv_sem=dsrecv.at[0],
                                          device_id=dev(mate), device_id_type=MESH)
    stcopy.start()

    @pl.loop(0, LAG)
    def _(i):
        mix(i)

    stcopy.wait()
    m0, l0, m1, l1 = st[core, :, 0, :], st[core, :, 1, :], stin[:, 0, :], stin[:, 1, :]
    top = jnp.maximum(m0, m1)
    f0, f1 = jnp.exp(m0 - top), jnp.exp(m1 - top)
    fac[0], fac[1] = f0, f1
    stsend[:, 0, :] = top
    stsend[:, 1, :] = l0 * f0 + l1 * f1

    @pl.loop(1, CHIPS)
    def _(off):
        s = lax.rem(chip + off, CHIPS)
        pltpu.make_async_remote_copy(src_ref=stsend.at[s // 8], dst_ref=rst.at[chip], send_sem=tsend.at[0], recv_sem=trecv.at[0],
                                     device_id=dev(s * 2 + core), device_id_type=MESH).start()

    @pl.loop(LAG, 8 + LAG)
    def _(i):
        @pl.when(i < 8)
        def _():
            mix(i)

        merge(i - LAG)

    rst[chip] = stsend[chip // 8]
    rbuf[chip] = osend[chip]

    def all_of(src, dst, send, recv):
        return pltpu.make_async_remote_copy(src_ref=src, dst_ref=dst, send_sem=send, recv_sem=recv, device_id=dev(mate),
                                            device_id_type=MESH)

    others = pl.ds(0, CHIPS - 1)
    all_of(rst.at[others], rst.at[others], tsend.at[0], trecv.at[0]).wait_recv()
    all_of(rbuf.at[others], rbuf.at[others], ssend.at[0], srecv.at[0]).wait_recv()

    here = lane16 == lax.rem(chip, 8) * HALF + row16
    tops = rst[:, 0, :]
    top = jnp.max(tops, axis=0, keepdims=True)
    facs = jnp.exp(tops - top)
    total = pick(jnp.sum(rst[:, 1, :] * facs, axis=0, keepdims=True), here)
    acc = jnp.zeros((HALF, HEAD_DIM), F32)
    for c in range(CHIPS):
        acc += rbuf[c] * pick(facs[c:c + 1], here)
    q_own = jnp.concatenate([gbuf[2 * core, chip], gbuf[2 * core + 1, chip]], axis=0)
    kv_own = gbuf[4 + core, chip]
    k_own = jnp.concatenate([jnp.broadcast_to(kv_own[i:i + 1], (4, HEAD_DIM)) for i in range(4)], axis=0)
    v_own = jnp.concatenate([jnp.broadcast_to(kv_own[4 + i:5 + i], (4, HEAD_DIM)) for i in range(4)], axis=0)
    s_own = jnp.sum(q_own * k_own, axis=-1, keepdims=True) * SCALE
    top = pick(top, here)
    peak = jnp.maximum(top, s_own)
    f_old, f_new = jnp.exp(top - peak), jnp.exp(s_own - peak)
    attn = (acc * f_old + v_own * f_new) / (total * f_old + f_new)
    for h in range(HALF):
        lhs[:, h * 128:(h + 1) * 128] = jnp.where(row16 == h, attn, 0.0).astype(BF16)

    wocopy.wait()

    def out_cols(half, slot):
        for n in range(5):
            cols = pl.ds(pl.multiple_of(half * 1280 + n * 256, 256), 256)
            res = jnp.dot(lhs[...], wobuf[:, cols], preferred_element_type=F32)
            res = jnp.sum(res, axis=0, keepdims=True)
            for k in range(2):
                ypart[slot, pl.ds(2 * n + k, 1), :] = res[:, k * 128:(k + 1) * 128]

    out_cols(1 - core, 0)
    ycopy = pltpu.make_async_remote_copy(src_ref=ypart.at[0], dst_ref=yin, send_sem=ysem.at[0], recv_sem=ysem.at[1],
                                         device_id=dev(mate), device_id_type=MESH)
    ycopy.start()
    out_cols(core, 1)
    ycopy.wait()
    ysend[...] = ypart[1] + yin[...]

    def bcopy(s, group):
        return pltpu.make_async_remote_copy(src_ref=ysend, dst_ref=ybuf.at[core, chip], send_sem=bsend.at[0],
                                            recv_sem=brecv.at[group], device_id=dev(s * 2 + core), device_id_type=MESH)

    @pl.loop(1, CHIPS)
    def _(k):
        s = lax.rem(chip + 1 + lax.rem(k + 30, CHIPS - 1), CHIPS)
        bcopy(s, lax.rem(zed - s // 16 + 4, 4)).start()

    ybuf[core, chip] = ysend[...]

    def slab(half, group):
        return ybuf.at[half, pl.ds(lax.rem(zed + group, 4) * 16, 16)]

    def fcopy(half, group):
        ref = slab(half, group)
        return pltpu.make_async_remote_copy(src_ref=ref, dst_ref=ref, send_sem=fsend.at[group], recv_sem=frecv.at[group],
                                            device_id=dev(mate), device_id_type=MESH)

    for group in (0, 1, 3, 2):
        ref = ybuf.at[core, pl.ds(0, 15 if group == 0 else 16)]
        all_of(ref, ref, bsend.at[0], brecv.at[group]).wait_recv()
        fcopy(core, group).start()
    for group in (0, 1, 3, 2):
        fcopy(1 - core, group).wait_recv()

    for half in range(2):
        for k in range(10):
            cols = slice(half * 1280 + k * 128, half * 1280 + (k + 1) * 128)
            out_ref[:, cols] = (tok_ref[:, cols].astype(F32) + ybuf[half, :, k, :]).astype(BF16)

    outcopy = pltpu.make_async_copy(out_ref, out_hbm, outsem.at[0])
    outcopy.start()
    for group in range(4):
        fcopy(core, group).wait_send()
    all_of(rst.at[others], rst.at[others], tsend.at[0], trecv.at[0]).wait_send()
    all_of(rbuf.at[others], rbuf.at[others], ssend.at[0], srecv.at[0]).wait_send()
    rest = ybuf.at[0, others]
    all_of(rest, rest, bsend.at[0], brecv.at[0]).wait_send()
    kvout.wait()
    outcopy.wait()


def step_call(*args):
    dma = pltpu.SemaphoreType.DMA
    vmem = pltpu.VMEM
    hbm = pl.BlockSpec(memory_space=pl.ANY)
    return pl.pallas_call(
        step_kernel,
        name="decode_step",
        out_shape=(jax.ShapeDtypeStruct((SEQS, DIM), BF16), jax.ShapeDtypeStruct((2, SEQS, 8, HEAD_DIM), F32)),
        in_specs=[pl.BlockSpec(memory_space=pltpu.SMEM)] + [hbm] * 11,
        out_specs=(hbm, hbm),
        scratch_shapes=[
            vmem((SEQS, DIM), BF16), vmem((DIM,), BF16), vmem((1, HEAD_DIM), BF16), vmem((1, HEAD_DIM), BF16), vmem((1, HEAD_DIM), F32),
            dma((5,)), dma((1,)),
            vmem((SEQS, DIM), BF16), vmem((SEQS, HEAD_DIM), F32), vmem((SEQS, HEAD_DIM), F32),
            vmem((12, DIM, 256), BF16), vmem((2048, DIM), BF16),
            vmem((SEQS, 128, HEAD_DIM), BF16), vmem((SEQS, 128, HEAD_DIM), BF16),
            vmem((6, SEQS, 8, HEAD_DIM), F32),
            vmem((SEQS, HEADS, HEAD_DIM), BF16), vmem((2, SEQS, HALF, HEAD_DIM), F32), vmem((SEQS, HALF, HEAD_DIM), F32),
            vmem((2, 8, 2, HEAD_DIM), F32), vmem((8, 2, HEAD_DIM), F32), vmem((2, 8, HEAD_DIM), F32),
            vmem((SEQS, HALF, HEAD_DIM), F32), vmem((8, 2, HEAD_DIM), F32),
            vmem((CHIPS, HALF, HEAD_DIM), F32), vmem((CHIPS, 2, HEAD_DIM), F32), vmem((SEQS, DIM), BF16),
            vmem((HALF, 2048), BF16), vmem((2, 10, HEAD_DIM), F32), vmem((10, HEAD_DIM), F32), vmem((10, HEAD_DIM), F32),
            vmem((2, CHIPS, 10, HEAD_DIM), F32),
            dma((12,)), dma((1,)), dma((2, 4)), dma((1,)), dma((3,)), dma((3,)), dma((8,)), dma((8,)), dma((1,)), dma((1,)),
            dma((1,)), dma((1,)), dma((1,)), dma((1,)), dma((2,)), dma((1,)), dma((4,)), dma((4,)), dma((4,)),
        ],
        compiler_params=pltpu.CompilerParams(collective_id=0, has_side_effects=True, vmem_limit_bytes=60 * 2 ** 20),
    )(*args)


CHUNKS = 8


def cache_kernel(pos_ref, kv_hbm, row_hbm, kc_hbm, vc_hbm, ko_hbm, vo_hbm, new_hbm, out_hbm,
                 kv, new, row, kbuf, vbuf, isem, osem, ssem):
    start = lax.axis_index("sp") * SLOTS
    per = SEQS // CHUNKS

    def copies(i, out):
        rows = pl.ds(i * per, per)
        if out:
            return (pltpu.make_async_copy(kbuf.at[rows], ko_hbm.at[rows], osem.at[0, i]),
                    pltpu.make_async_copy(vbuf.at[rows], vo_hbm.at[rows], osem.at[1, i]))
        return (pltpu.make_async_copy(kc_hbm.at[rows], kbuf.at[rows], isem.at[0, i]),
                pltpu.make_async_copy(vc_hbm.at[rows], vbuf.at[rows], isem.at[1, i]))

    kvload, rowload = pltpu.make_async_copy(kv_hbm, kv, ssem.at[0]), pltpu.make_async_copy(row_hbm, row, ssem.at[1])
    kvload.start()
    rowload.start()
    for i in range(CHUNKS):
        for c in copies(i, False):
            c.start()
    kvload.wait()
    low = iota((SEQS, 8, HEAD_DIM), 1) < 4
    first, second = kv[0], kv[1]
    new[:, 0] = jnp.where(low, first, pltpu.roll(second, 4, 1)).astype(BF16)
    new[:, 1] = jnp.where(low, pltpu.roll(first, 4, 1), second).astype(BF16)
    small = [pltpu.make_async_copy(new, new_hbm, ssem.at[2]), pltpu.make_async_copy(row, out_hbm, ssem.at[3])]
    small[0].start()
    rowload.wait()
    small[1].start()
    for i in range(CHUNKS):
        for c in copies(i, False):
            c.wait()

        @pl.loop(i * per, (i + 1) * per)
        def _(s):
            slot = pos_ref[s] - start

            @pl.when((slot >= 0) & (slot < SLOTS))
            def _():
                kbuf[s, slot] = new[s, 0]
                vbuf[s, slot] = new[s, 1]

        for c in copies(i, True):
            c.start()
    for c in small:
        c.wait()
    for i in range(CHUNKS):
        for c in copies(i, True):
            c.wait()


def cache_call(*args):
    hbm = pl.BlockSpec(memory_space=pl.ANY)
    shape = (SEQS, SLOTS, KV_HEADS, HEAD_DIM)
    new = (SEQS, 2, KV_HEADS, HEAD_DIM)
    dma = pltpu.SemaphoreType.DMA
    return pl.pallas_call(
        cache_kernel,
        name="cache_write",
        out_shape=(jax.ShapeDtypeStruct(shape, BF16), jax.ShapeDtypeStruct(shape, BF16), jax.ShapeDtypeStruct(new, BF16),
                   jax.ShapeDtypeStruct((SEQS, DIM), BF16)),
        in_specs=[pl.BlockSpec(memory_space=pltpu.SMEM)] + [hbm] * 4,
        out_specs=(hbm,) * 4,
        scratch_shapes=[pltpu.VMEM((2, SEQS, 8, HEAD_DIM), F32), pltpu.VMEM(new, BF16), pltpu.VMEM((SEQS, DIM), BF16),
                        pltpu.VMEM(shape, BF16), pltpu.VMEM(shape, BF16), dma((2, CHUNKS)), dma((2, CHUNKS)), dma((4,))],
    )(*args)


def solution(mesh):
    cache_spec = P('dp', 'sp', None, None)

    def device_step(tokens, positions, k_cache, v_cache, w_q, w_k, w_v, w_o, attn_norm, q_norm, k_norm):
        inv = np.float32(ROPE_THETA) ** (-np.arange(HEAD_DIM // 2, dtype=np.float32) * np.float32(2.0) / np.float32(HEAD_DIM))
        freq = jnp.asarray(np.concatenate([inv, inv])[None, :].astype(np.float32))
        flat = (SEQS, SLOTS * KV_HEADS, HEAD_DIM)
        row, kv = step_call(positions, tokens, attn_norm, q_norm[None, :], k_norm[None, :], freq, w_q, w_k, w_v,
                                  w_o, k_cache.reshape(flat), v_cache.reshape(flat))
        k_out, v_out, new_kv, block_out = cache_call(positions, kv, row, k_cache, v_cache)
        return block_out, k_out, v_out, new_kv

    return jax.shard_map(device_step, mesh=mesh, in_specs=(P('dp', None), P('dp'), cache_spec, cache_spec, P(), P(), P(), P(), P(), P(), P()), out_specs=(P('dp', None), cache_spec, cache_spec, P('dp', None, None, None)), check_vma=False)
```

time: 66.1 us -> 53.8 us (0.81)
  Pallas kernels: 62.2 us -> 53 us
  local copies, waits for them, and re-layouts: 3.02 us -> 0 us
    pallas_call x1, Pallas kernels: 56.7 us -> 47.6 us  [step_call(): pl.pallas_call(step_kernel, name='decode_step', out_shape=(jax.ShapeDtype...]
    unnamed x1 -> x0, local copies, waits for them, and re-layouts: 1.72 us -> none
    broadcast_in_dim x1 -> x0, local copies, waits for them, and re-layouts: 1.3 us -> none  [device_step(): attn_norm[None, :]]
where the time goes in v2:
time: 53.8 us; the launch traced here: 53.6 us
  Pallas kernels  53 us (99%)
  between operations  0.64 us (1%)
    pallas_call x1, Pallas kernels, step_call(): pl.pallas_call(step_kernel, name='decode_step', out_shape=(jax.ShapeDtype...  47.6 us
    pallas_call x1, Pallas kernels, cache_call(): pl.pallas_call(cache_kernel, name='cache_write', out_shape=(jax.ShapeDtyp...  5.39 us

profile of v2, /device:TPU:1, one launch (start us, length us, event | category | flops | bytes accessed | tf_op | source)
XLA Modules:
  0.0 53.6 jit_solution(14959529756764303757)
XLA Ops:
  0.6 47.6 %decode_step.1 = (bf16[64,2560]{1,0:T(8,128)(2,1)}, f32[2,64,8,128]{3,2,1,0:T(8,128)}) custom-call(s32[64]{0:T(128)} %pos_ref.3, bf16[64,2560]{1,0:T(8,128)(2,1)} %tok_hbm.1, bf16[2560]{0:T(1024)(128)(2,1)} %an_hbm.1, bf16[1,128]{1,0:T(2,128)(2,1)} %bitcast.6, bf16[1,128]{1,0:T(2,128)(2,1)} %bitcast.7, f32[1,128]{1,0:T(1,128)} %constant.2.clone.freq_hbm, ...), custom_call_target="tpu_custom_call" | custom-call | tf_op jit(solution)/shard_map/decode_step/pallas_call | solution.py:331
  48.2 5.4 %cache_write.1 = (bf16[64,16,8,128]{3,2,1,0:T(8,128)(2,1)}, bf16[64,16,8,128]{3,2,1,0:T(8,128)(2,1)}, bf16[64,2,8,128]{3,2,1,0:T(8,128)(2,1)}, bf16[64,2560]{1,0:T(8,128)(2,1)}) custom-call(s32[64]{0:T(128)} %pos_ref.3, f32[2,64,8,128]{3,2,1,0:T(8,128)} %get-tuple-element.10.kv_hbm, bf16[64,2560]{1,0:T(8,128)(2,1)} %get-tuple-element.11.row_hbm, ...), custom_call_target="tpu_custom_call" | custom-call | tf_op jit(solution)/shard_map/cache_write/pallas_call | solution.py:415

commit v3 on v2

--- a/solution.py
+++ b/solution.py
@@ -35,8 +35,8 @@
 
 
 def step_kernel(pos_ref, tok_hbm, an_hbm, qn_hbm, kn_hbm, freq_hbm, wq_hbm, wk_hbm, wv_hbm, wo_hbm, kc_hbm, vc_hbm,
-                out_hbm, kv_hbm,
-                tok_ref, an_ref, qn_ref, kn_ref, freq_ref, isem, outsem, hid, cosr, sinr, wbuf, wobuf, kbuf, vbuf, gbuf, wts, obuf, oin, st, stin, fac, osend, stsend, rbuf, rst, out_ref,
+                out_hbm, kv_hbm, kbuf, vbuf,
+                tok_ref, an_ref, qn_ref, kn_ref, freq_ref, isem, outsem, hid, cosr, sinr, wbuf, wobuf, gbuf, wts, obuf, oin, st, stin, fac, osend, stsend, rbuf, rst, out_ref,
                 lhs, ypart, yin, ysend, ybuf,
                 wsem, wosem, csem, kvsem, gsend, grecv, dsend, drecv, dssend, dsrecv,
                 ssend, srecv, tsend, trecv, ysem, bsend, brecv, fsend, frecv):
@@ -140,7 +140,7 @@
             c.wait()
 
     def block_of(i):
-        return lax.rem(zed + 2 + 3 * (i // 2), 4) * 2 + lax.rem(i, 2)
+        return lax.rem(zed + 2 + i // 2 - (i // 4) * (2 * (i // 2) - 1), 4) * 2 + lax.rem(i, 2)
 
     row32, col32 = iota((HEADS, HEAD_DIM), 0), iota((HEADS, HEAD_DIM), 1)
     same_head = (col32 % KV_HEADS) == (row32 // 4)
@@ -328,18 +328,19 @@
     dma = pltpu.SemaphoreType.DMA
     vmem = pltpu.VMEM
     hbm = pl.BlockSpec(memory_space=pl.ANY)
+    vm = pl.BlockSpec(memory_space=pltpu.VMEM)
     return pl.pallas_call(
         step_kernel,
         name="decode_step",
-        out_shape=(jax.ShapeDtypeStruct((SEQS, DIM), BF16), jax.ShapeDtypeStruct((2, SEQS, 8, HEAD_DIM), F32)),
-        in_specs=[pl.BlockSpec(memory_space=pltpu.SMEM)] + [hbm] * 11,
-        out_specs=(hbm, hbm),
+        out_shape=(jax.ShapeDtypeStruct((SEQS, DIM), BF16), jax.ShapeDtypeStruct((2, SEQS, 8, HEAD_DIM), F32),
+                   jax.ShapeDtypeStruct((SEQS, 128, HEAD_DIM), BF16), jax.ShapeDtypeStruct((SEQS, 128, HEAD_DIM), BF16)),
+        in_specs=[pl.BlockSpec(memory_space=pltpu.SMEM)] + [pl.BlockSpec(memory_space=pltpu.HBM)] * 11,
+        out_specs=(hbm, hbm, vm, vm),
         scratch_shapes=[
             vmem((SEQS, DIM), BF16), vmem((DIM,), BF16), vmem((1, HEAD_DIM), BF16), vmem((1, HEAD_DIM), BF16), vmem((1, HEAD_DIM), F32),
             dma((5,)), dma((1,)),
             vmem((SEQS, DIM), BF16), vmem((SEQS, HEAD_DIM), F32), vmem((SEQS, HEAD_DIM), F32),
             vmem((12, DIM, 256), BF16), vmem((2048, DIM), BF16),
-            vmem((SEQS, 128, HEAD_DIM), BF16), vmem((SEQS, 128, HEAD_DIM), BF16),
             vmem((6, SEQS, 8, HEAD_DIM), F32),
             vmem((SEQS, HEADS, HEAD_DIM), BF16), vmem((2, SEQS, HALF, HEAD_DIM), F32), vmem((SEQS, HALF, HEAD_DIM), F32),
             vmem((2, 8, 2, HEAD_DIM), F32), vmem((8, 2, HEAD_DIM), F32), vmem((2, 8, HEAD_DIM), F32),
@@ -350,32 +351,26 @@
             dma((12,)), dma((1,)), dma((2, 4)), dma((1,)), dma((3,)), dma((3,)), dma((8,)), dma((8,)), dma((1,)), dma((1,)),
             dma((1,)), dma((1,)), dma((1,)), dma((1,)), dma((2,)), dma((1,)), dma((4,)), dma((4,)), dma((4,)),
         ],
-        compiler_params=pltpu.CompilerParams(collective_id=0, has_side_effects=True, vmem_limit_bytes=60 * 2 ** 20),
+        compiler_params=pltpu.CompilerParams(collective_id=0, has_side_effects=True, vmem_limit_bytes=48 * 2 ** 20),
     )(*args)
 
 
 CHUNKS = 8
 
 
-def cache_kernel(pos_ref, kv_hbm, row_hbm, kc_hbm, vc_hbm, ko_hbm, vo_hbm, new_hbm, out_hbm,
-                 kv, new, row, kbuf, vbuf, isem, osem, ssem):
+def cache_kernel(pos_ref, kv_hbm, row_hbm, kbuf, vbuf, ko_hbm, vo_hbm, new_hbm, out_hbm,
+                 kv, new, row, osem, ssem):
     start = lax.axis_index("sp") * SLOTS
     per = SEQS // CHUNKS
 
-    def copies(i, out):
+    def copies(i):
         rows = pl.ds(i * per, per)
-        if out:
-            return (pltpu.make_async_copy(kbuf.at[rows], ko_hbm.at[rows], osem.at[0, i]),
-                    pltpu.make_async_copy(vbuf.at[rows], vo_hbm.at[rows], osem.at[1, i]))
-        return (pltpu.make_async_copy(kc_hbm.at[rows], kbuf.at[rows], isem.at[0, i]),
-                pltpu.make_async_copy(vc_hbm.at[rows], vbuf.at[rows], isem.at[1, i]))
+        return (pltpu.make_async_copy(kbuf.at[rows], ko_hbm.at[rows], osem.at[0, i]),
+                pltpu.make_async_copy(vbuf.at[rows], vo_hbm.at[rows], osem.at[1, i]))
 
     kvload, rowload = pltpu.make_async_copy(kv_hbm, kv, ssem.at[0]), pltpu.make_async_copy(row_hbm, row, ssem.at[1])
     kvload.start()
     rowload.start()
-    for i in range(CHUNKS):
-        for c in copies(i, False):
-            c.start()
     kvload.wait()
     low = iota((SEQS, 8, HEAD_DIM), 1) < 4
     first, second = kv[0], kv[1]
@@ -386,9 +381,6 @@
     rowload.wait()
     small[1].start()
     for i in range(CHUNKS):
-        for c in copies(i, False):
-            c.wait()
-
         @pl.loop(i * per, (i + 1) * per)
         def _(s):
             slot = pos_ref[s] - start
@@ -398,12 +390,12 @@
                 kbuf[s, slot] = new[s, 0]
                 vbuf[s, slot] = new[s, 1]
 
-        for c in copies(i, True):
+        for c in copies(i):
             c.start()
     for c in small:
         c.wait()
     for i in range(CHUNKS):
-        for c in copies(i, True):
+        for c in copies(i):
             c.wait()
 
 
@@ -417,10 +409,11 @@
         name="cache_write",
         out_shape=(jax.ShapeDtypeStruct(shape, BF16), jax.ShapeDtypeStruct(shape, BF16), jax.ShapeDtypeStruct(new, BF16),
                    jax.ShapeDtypeStruct((SEQS, DIM), BF16)),
-        in_specs=[pl.BlockSpec(memory_space=pltpu.SMEM)] + [hbm] * 4,
+        in_specs=[pl.BlockSpec(memory_space=pltpu.SMEM)] + [hbm] * 2 + [pl.BlockSpec(memory_space=pltpu.VMEM)] * 2,
+        compiler_params=pltpu.CompilerParams(vmem_limit_bytes=12 * 2 ** 20),
         out_specs=(hbm,) * 4,
         scratch_shapes=[pltpu.VMEM((2, SEQS, 8, HEAD_DIM), F32), pltpu.VMEM(new, BF16), pltpu.VMEM((SEQS, DIM), BF16),
-                        pltpu.VMEM(shape, BF16), pltpu.VMEM(shape, BF16), dma((2, CHUNKS)), dma((2, CHUNKS)), dma((4,))],
+                        dma((2, CHUNKS)), dma((4,))],
     )(*args)
 
 
@@ -431,9 +424,9 @@
         inv = np.float32(ROPE_THETA) ** (-np.arange(HEAD_DIM // 2, dtype=np.float32) * np.float32(2.0) / np.float32(HEAD_DIM))
         freq = jnp.asarray(np.concatenate([inv, inv])[None, :].astype(np.float32))
         flat = (SEQS, SLOTS * KV_HEADS, HEAD_DIM)
-        row, kv = step_call(positions, tokens, attn_norm, q_norm[None, :], k_norm[None, :], freq, w_q, w_k, w_v,
+        row, kv, k_loc, v_loc = step_call(positions, tokens, attn_norm, q_norm[None, :], k_norm[None, :], freq, w_q, w_k, w_v,
                                   w_o, k_cache.reshape(flat), v_cache.reshape(flat))
-        k_out, v_out, new_kv, block_out = cache_call(positions, kv, row, k_cache, v_cache)
+        k_out, v_out, new_kv, block_out = cache_call(positions, kv, row, k_loc.reshape(k_cache.shape), v_loc.reshape(v_cache.shape))
         return block_out, k_out, v_out, new_kv
 
     return jax.shard_map(device_step, mesh=mesh, in_specs=(P('dp', None), P('dp'), cache_spec, cache_spec, P(), P(), P(), P(), P(), P(), P()), out_specs=(P('dp', None), cache_spec, cache_spec, P('dp', None, None, None)), check_vma=False)

time: 53.8 us -> 53.6 us (level)
  Pallas kernels: 53 us -> 48.5 us
  local copies, waits for them, and re-layouts: 0 us -> 4.28 us
    unnamed x0 -> x12, local copies, waits for them, and re-layouts: none -> 4.28 us
    pallas_call x1, Pallas kernels: 5.39 us -> 3.1 us  [cache_call(): pl.pallas_call(cache_kernel, name='cache_write', out_shape=(jax.ShapeDtyp...]
    pallas_call x1, Pallas kernels: 47.6 us -> 45.4 us  [step_call(): pl.pallas_call(step_kernel, name='decode_step', out_shape=(jax.ShapeDtype...]
where the time goes in v3:
time: 53.6 us; the launch traced here: 53.4 us
  Pallas kernels  48.5 us (90%)
  local copies, waits for them, and re-layouts  4.28 us (8%)
  between operations  0.66 us (1%)
    pallas_call x1, Pallas kernels, step_call(): pl.pallas_call(step_kernel, name='decode_step', out_shape=(jax.ShapeDtype...  45.4 us
    unnamed x12, local copies, waits for them, and re-layouts  4.28 us
    pallas_call x1, Pallas kernels, cache_call(): pl.pallas_call(cache_kernel, name='cache_write', out_shape=(jax.ShapeDtyp...  3.1 us

profile of v3, /device:TPU:1, one launch (start us, length us, event | category | flops | bytes accessed | tf_op | source)
XLA Modules:
  0.0 53.4 jit_solution(12025935576789424261)
XLA Ops:
  0.6 0.0 copy-start
  0.6 1.0 %copy-done = bf16[64,2560]{1,0:T(8,128)(2,1)S(1)} copy-done((bf16[64,2560]{1,0:T(8,128)(2,1)S(1)}, bf16[64,2560]{1,0:T(8,128)(2,1)}, u32[]{:S(2)}) %copy-start) | copy-done | bytes 327704
  1.6 0.0 copy-start.1
  1.6 0.7 %copy-done.1 = bf16[2560]{0:T(1024)(128)(2,1)S(1)} copy-done((bf16[2560]{0:T(1024)(128)(2,1)S(1)}, bf16[2560]{0:T(1024)(128)(2,1)}, u32[]{:S(2)}) %copy-start.1) | copy-done | bytes 5144
  2.3 0.0 copy-start.2
  2.3 0.7 %copy-done.2 = s32[64]{0:T(128)S(1)} copy-done((s32[64]{0:T(128)S(1)}, s32[64]{0:T(128)}, u32[]{:S(2)}) %copy-start.2) | copy-done | bytes 280
  3.0 0.0 copy-start.3
  3.0 0.7 %copy-done.3 = bf16[128]{0:T(256)(128)(2,1)S(1)} copy-done((bf16[128]{0:T(256)(128)(2,1)S(1)}, bf16[128]{0:T(256)(128)(2,1)}, u32[]{:S(2)}) %copy-start.3) | copy-done | bytes 280
  3.6 0.0 copy-start.4
  3.6 0.7 %copy-done.4 = bf16[128]{0:T(256)(128)(2,1)S(1)} copy-done((bf16[128]{0:T(256)(128)(2,1)S(1)}, bf16[128]{0:T(256)(128)(2,1)}, u32[]{:S(2)}) %copy-start.4) | copy-done | bytes 280
  4.3 0.0 copy-start.5
  4.3 0.7 %copy-done.5 = f32[1,128]{1,0:T(1,128)S(1)} copy-done((f32[1,128]{1,0:T(1,128)S(1)}, f32[1,128]{1,0:T(1,128)}, u32[]{:S(2)}) %copy-start.5) | copy-done | bytes 536
  4.9 45.4 %decode_step.1 = (bf16[64,2560]{1,0:T(8,128)(2,1)S(1)}, f32[2,64,8,128]{3,2,1,0:T(8,128)S(1)}, bf16[64,128,128]{2,1,0:T(8,128)(2,1)S(1)}, bf16[64,128,128]{2,1,0:T(8,128)(2,1)S(1)}) custom-call(s32[64]{0:T(128)S(1)} %copy-done.2, bf16[64,2560]{1,0:T(8,128)(2,1)S(1)} %copy-done, bf16[2560]{0:T(1024)(128)(2,1)S(1)} %copy-done.1, bf16[1,128]{1,0:T(2,128)(2,1)S(1)} %bitcast.8, ...), custom_call_target="tpu_custom_call" | custom-call | tf_op jit(solution)/shard_map/decode_step/pallas_call | solution.py:332
  50.3 3.1 %cache_write.1 = (bf16[64,16,8,128]{3,2,1,0:T(8,128)(2,1)}, bf16[64,16,8,128]{3,2,1,0:T(8,128)(2,1)}, bf16[64,2,8,128]{3,2,1,0:T(8,128)(2,1)}, bf16[64,2560]{1,0:T(8,128)(2,1)}) custom-call(s32[64]{0:T(128)S(1)} %copy-done.2, f32[2,64,8,128]{3,2,1,0:T(8,128)S(1)} %get-tuple-element.12.kv_hbm, bf16[64,2560]{1,0:T(8,128)(2,1)S(1)} %get-tuple-element.13.row_hbm, ...), custom_call_target="tpu_custom_call" | custom-call | tf_op jit(solution)/shard_map/cache_write/pallas_call | solution.py:407
Async XLA Ops:
  0.6 1.0 %copy-start = (bf16[64,2560]{1,0:T(8,128)(2,1)S(1)}, bf16[64,2560]{1,0:T(8,128)(2,1)}, u32[]{:S(2)}) copy-start(bf16[64,2560]{1,0:T(8,128)(2,1)} %tok_hbm.1) | copy-start | bytes 983044
  1.6 0.7 %copy-start.1 = (bf16[2560]{0:T(1024)(128)(2,1)S(1)}, bf16[2560]{0:T(1024)(128)(2,1)}, u32[]{:S(2)}) copy-start(bf16[2560]{0:T(1024)(128)(2,1)} %an_hbm.1) | copy-start | bytes 15364
  2.3 0.7 %copy-start.2 = (s32[64]{0:T(128)S(1)}, s32[64]{0:T(128)}, u32[]{:S(2)}) copy-start(s32[64]{0:T(128)} %pos_ref.3) | copy-start | bytes 772
  3.0 0.7 %copy-start.3 = (bf16[128]{0:T(256)(128)(2,1)S(1)}, bf16[128]{0:T(256)(128)(2,1)}, u32[]{:S(2)}) copy-start(bf16[128]{0:T(256)(128)(2,1)} %param.21) | copy-start | bytes 772
  3.6 0.7 %copy-start.4 = (bf16[128]{0:T(256)(128)(2,1)S(1)}, bf16[128]{0:T(256)(128)(2,1)}, u32[]{:S(2)}) copy-start(bf16[128]{0:T(256)(128)(2,1)} %param.22) | copy-start | bytes 772
  4.3 0.7 %copy-start.5 = (f32[1,128]{1,0:T(1,128)S(1)}, f32[1,128]{1,0:T(1,128)}, u32[]{:S(2)}) copy-start(f32[1,128]{1,0:T(1,128)} %constant.2.clone.freq_hbm) | copy-start | bytes 1540

commit v4 on v3

--- a/solution.py
+++ b/solution.py
@@ -34,11 +34,11 @@
     return jnp.sum(jnp.where(lane, spread, 0.0), axis=-1, keepdims=True)
 
 
-def step_kernel(pos_ref, tok_hbm, an_hbm, qn_hbm, kn_hbm, freq_hbm, wq_hbm, wk_hbm, wv_hbm, wo_hbm, kc_hbm, vc_hbm,
-                out_hbm, kv_hbm, kbuf, vbuf,
-                tok_ref, an_ref, qn_ref, kn_ref, freq_ref, isem, outsem, hid, cosr, sinr, wbuf, wobuf, gbuf, wts, obuf, oin, st, stin, fac, osend, stsend, rbuf, rst, out_ref,
+def step_kernel(pos_hbm, tok_hbm, an_hbm, qn_hbm, kn_hbm, freq_hbm, wq_hbm, wk_hbm, wv_hbm, wo_hbm, kc_hbm, vc_hbm,
+                out_ref, new_ref, kbuf, vbuf,
+                pos_ref, tok_ref, an_ref, qn_ref, kn_ref, freq_ref, isem, facbuf, hid, cosr, sinr, wbuf, wobuf, gbuf, wts, obuf, oin, st, stin, fac, osend, stsend, rbuf, rst,
                 lhs, ypart, yin, ysend, ybuf,
-                wsem, wosem, csem, kvsem, gsend, grecv, dsend, drecv, dssend, dsrecv,
+                wsem, wosem, csem, gsend, grecv, dsend, drecv, dssend, dsrecv,
                 ssend, srecv, tsend, trecv, ysem, bsend, brecv, fsend, frecv):
     me = lax.axis_index("sp")
     chip, core = me // 2, me % 2
@@ -48,13 +48,6 @@
 
     def dev(index):
         return (lax.axis_index("dp"), index)
-
-    barrier = pltpu.get_barrier_semaphore()
-    pl.semaphore_signal(barrier, inc=1, device_id=dev(mate), device_id_type=MESH)
-
-    @pl.loop(1, CHIPS)
-    def _(off):
-        pl.semaphore_signal(barrier, inc=1, device_id=dev(lax.rem(chip + off, CHIPS) * 2 + core), device_id_type=MESH)
 
     def wcopy(src, col, tile):
         return pltpu.make_async_copy(src.at[:, pl.ds(pl.multiple_of(col, 256), 256)], wbuf.at[tile], wsem.at[tile])
@@ -80,11 +73,18 @@
                 c.start()
 
     inputs = [pltpu.make_async_copy(a, b, isem.at[i]) for i, (a, b) in enumerate(
-        [(tok_hbm, tok_ref), (an_hbm, an_ref), (freq_hbm, freq_ref), (kn_hbm, kn_ref), (qn_hbm, qn_ref)])]
+        [(tok_hbm, tok_ref), (an_hbm, an_ref), (pos_hbm, pos_ref), (freq_hbm, freq_ref), (kn_hbm, kn_ref), (qn_hbm, qn_ref)])]
     for c in inputs:
         c.start()
     for t in range(DEPTH):
         tile_copy(t).start()
+    barrier = pltpu.get_barrier_semaphore()
+    pl.semaphore_signal(barrier, inc=1, device_id=dev(mate), device_id_type=MESH)
+
+    @pl.loop(1, CHIPS)
+    def _(off):
+        pl.semaphore_signal(barrier, inc=1, device_id=dev(lax.rem(chip + off, CHIPS) * 2 + core), device_id_type=MESH)
+
     for c in inputs:
         c.wait()
 
@@ -133,8 +133,6 @@
     wocopy.start()
     for slot in range(3):
         gcopy(4 + core if slot == 2 else 2 * core + slot, slot).wait()
-    kvout = pltpu.make_async_copy(gbuf.at[pl.ds(4, 2)], kv_hbm, kvsem.at[0])
-    kvout.start()
     for i in range(4):
         for c in kvload(i):
             c.wait()
@@ -195,7 +193,7 @@
 
             @pl.when(s != chip)
             def _():
-                pltpu.make_async_remote_copy(src_ref=osend.at[s], dst_ref=rbuf.at[chip], send_sem=ssend.at[0], recv_sem=srecv.at[0],
+                pltpu.make_async_remote_copy(src_ref=osend.at[s], dst_ref=rbuf.at[chip], send_sem=ssend.at[0], recv_sem=srecv.at[lax.rem(zed - s // 16 + 4, 4)],
                                              device_id=dev(s * 2 + core), device_id_type=MESH).start()
 
     @pl.loop(0, 8)
@@ -239,18 +237,18 @@
         return pltpu.make_async_remote_copy(src_ref=src, dst_ref=dst, send_sem=send, recv_sem=recv, device_id=dev(mate),
                                             device_id_type=MESH)
 
+    low = iota((SEQS, 8, HEAD_DIM), 1) < 4
+    new_ref[:, 0] = jnp.where(low, gbuf[4], pltpu.roll(gbuf[5], 4, 1)).astype(BF16)
+    new_ref[:, 1] = jnp.where(low, pltpu.roll(gbuf[4], 4, 1), gbuf[5]).astype(BF16)
+
     others = pl.ds(0, CHIPS - 1)
     all_of(rst.at[others], rst.at[others], tsend.at[0], trecv.at[0]).wait_recv()
-    all_of(rbuf.at[others], rbuf.at[others], ssend.at[0], srecv.at[0]).wait_recv()
-
     here = lane16 == lax.rem(chip, 8) * HALF + row16
     tops = rst[:, 0, :]
     top = jnp.max(tops, axis=0, keepdims=True)
     facs = jnp.exp(tops - top)
+    facbuf[...] = facs
     total = pick(jnp.sum(rst[:, 1, :] * facs, axis=0, keepdims=True), here)
-    acc = jnp.zeros((HALF, HEAD_DIM), F32)
-    for c in range(CHIPS):
-        acc += rbuf[c] * pick(facs[c:c + 1], here)
     q_own = jnp.concatenate([gbuf[2 * core, chip], gbuf[2 * core + 1, chip]], axis=0)
     kv_own = gbuf[4 + core, chip]
     k_own = jnp.concatenate([jnp.broadcast_to(kv_own[i:i + 1], (4, HEAD_DIM)) for i in range(4)], axis=0)
@@ -259,6 +257,13 @@
     top = pick(top, here)
     peak = jnp.maximum(top, s_own)
     f_old, f_new = jnp.exp(top - peak), jnp.exp(s_own - peak)
+    acc = jnp.zeros((HALF, HEAD_DIM), F32)
+    for group in (0, 1, 3, 2):
+        part = rbuf.at[pl.ds(0, 15 if group == 0 else 16)]
+        all_of(part, part, ssend.at[0], srecv.at[group]).wait_recv()
+        base = lax.rem(zed + group, 4) * 16
+        for c in range(16):
+            acc += rbuf[base + c] * pick(facbuf[pl.ds(base + c, 1), :], here)
     attn = (acc * f_old + v_own * f_new) / (total * f_old + f_new)
     for h in range(HALF):
         lhs[:, h * 128:(h + 1) * 128] = jnp.where(row16 == h, attn, 0.0).astype(BF16)
@@ -312,44 +317,39 @@
             cols = slice(half * 1280 + k * 128, half * 1280 + (k + 1) * 128)
             out_ref[:, cols] = (tok_ref[:, cols].astype(F32) + ybuf[half, :, k, :]).astype(BF16)
 
-    outcopy = pltpu.make_async_copy(out_ref, out_hbm, outsem.at[0])
-    outcopy.start()
     for group in range(4):
         fcopy(core, group).wait_send()
     all_of(rst.at[others], rst.at[others], tsend.at[0], trecv.at[0]).wait_send()
     all_of(rbuf.at[others], rbuf.at[others], ssend.at[0], srecv.at[0]).wait_send()
     rest = ybuf.at[0, others]
     all_of(rest, rest, bsend.at[0], brecv.at[0]).wait_send()
-    kvout.wait()
-    outcopy.wait()
 
 
 def step_call(*args):
     dma = pltpu.SemaphoreType.DMA
     vmem = pltpu.VMEM
-    hbm = pl.BlockSpec(memory_space=pl.ANY)
     vm = pl.BlockSpec(memory_space=pltpu.VMEM)
     return pl.pallas_call(
         step_kernel,
         name="decode_step",
-        out_shape=(jax.ShapeDtypeStruct((SEQS, DIM), BF16), jax.ShapeDtypeStruct((2, SEQS, 8, HEAD_DIM), F32),
+        out_shape=(jax.ShapeDtypeStruct((SEQS, DIM), BF16), jax.ShapeDtypeStruct((SEQS, 2, KV_HEADS, HEAD_DIM), BF16),
                    jax.ShapeDtypeStruct((SEQS, 128, HEAD_DIM), BF16), jax.ShapeDtypeStruct((SEQS, 128, HEAD_DIM), BF16)),
-        in_specs=[pl.BlockSpec(memory_space=pltpu.SMEM)] + [pl.BlockSpec(memory_space=pltpu.HBM)] * 11,
-        out_specs=(hbm, hbm, vm, vm),
+        in_specs=[pl.BlockSpec(memory_space=pltpu.HBM)] * 12,
+        out_specs=(vm,) * 4,
         scratch_shapes=[
-            vmem((SEQS, DIM), BF16), vmem((DIM,), BF16), vmem((1, HEAD_DIM), BF16), vmem((1, HEAD_DIM), BF16), vmem((1, HEAD_DIM), F32),
-            dma((5,)), dma((1,)),
+            pltpu.SMEM((SEQS,), jnp.int32), vmem((SEQS, DIM), BF16), vmem((DIM,), BF16), vmem((1, HEAD_DIM), BF16), vmem((1, HEAD_DIM), BF16), vmem((1, HEAD_DIM), F32),
+            dma((6,)), vmem((CHIPS, HEAD_DIM), F32),
             vmem((SEQS, DIM), BF16), vmem((SEQS, HEAD_DIM), F32), vmem((SEQS, HEAD_DIM), F32),
             vmem((12, DIM, 256), BF16), vmem((2048, DIM), BF16),
             vmem((6, SEQS, 8, HEAD_DIM), F32),
             vmem((SEQS, HEADS, HEAD_DIM), BF16), vmem((2, SEQS, HALF, HEAD_DIM), F32), vmem((SEQS, HALF, HEAD_DIM), F32),
             vmem((2, 8, 2, HEAD_DIM), F32), vmem((8, 2, HEAD_DIM), F32), vmem((2, 8, HEAD_DIM), F32),
             vmem((SEQS, HALF, HEAD_DIM), F32), vmem((8, 2, HEAD_DIM), F32),
-            vmem((CHIPS, HALF, HEAD_DIM), F32), vmem((CHIPS, 2, HEAD_DIM), F32), vmem((SEQS, DIM), BF16),
+            vmem((CHIPS, HALF, HEAD_DIM), F32), vmem((CHIPS, 2, HEAD_DIM), F32),
             vmem((HALF, 2048), BF16), vmem((2, 10, HEAD_DIM), F32), vmem((10, HEAD_DIM), F32), vmem((10, HEAD_DIM), F32),
             vmem((2, CHIPS, 10, HEAD_DIM), F32),
-            dma((12,)), dma((1,)), dma((2, 4)), dma((1,)), dma((3,)), dma((3,)), dma((8,)), dma((8,)), dma((1,)), dma((1,)),
-            dma((1,)), dma((1,)), dma((1,)), dma((1,)), dma((2,)), dma((1,)), dma((4,)), dma((4,)), dma((4,)),
+            dma((12,)), dma((1,)), dma((2, 4)), dma((3,)), dma((3,)), dma((8,)), dma((8,)), dma((1,)), dma((1,)),
+            dma((1,)), dma((4,)), dma((1,)), dma((1,)), dma((2,)), dma((1,)), dma((4,)), dma((4,)), dma((4,)),
         ],
         compiler_params=pltpu.CompilerParams(collective_id=0, has_side_effects=True, vmem_limit_bytes=48 * 2 ** 20),
     )(*args)
@@ -358,28 +358,12 @@
 CHUNKS = 8
 
 
-def cache_kernel(pos_ref, kv_hbm, row_hbm, kbuf, vbuf, ko_hbm, vo_hbm, new_hbm, out_hbm,
-                 kv, new, row, osem, ssem):
+def cache_kernel(pos_ref, new, row, kbuf, vbuf, ko_hbm, vo_hbm, new_hbm, out_hbm, osem, ssem):
     start = lax.axis_index("sp") * SLOTS
     per = SEQS // CHUNKS
-
-    def copies(i):
-        rows = pl.ds(i * per, per)
-        return (pltpu.make_async_copy(kbuf.at[rows], ko_hbm.at[rows], osem.at[0, i]),
-                pltpu.make_async_copy(vbuf.at[rows], vo_hbm.at[rows], osem.at[1, i]))
-
-    kvload, rowload = pltpu.make_async_copy(kv_hbm, kv, ssem.at[0]), pltpu.make_async_copy(row_hbm, row, ssem.at[1])
-    kvload.start()
-    rowload.start()
-    kvload.wait()
-    low = iota((SEQS, 8, HEAD_DIM), 1) < 4
-    first, second = kv[0], kv[1]
-    new[:, 0] = jnp.where(low, first, pltpu.roll(second, 4, 1)).astype(BF16)
-    new[:, 1] = jnp.where(low, pltpu.roll(first, 4, 1), second).astype(BF16)
-    small = [pltpu.make_async_copy(new, new_hbm, ssem.at[2]), pltpu.make_async_copy(row, out_hbm, ssem.at[3])]
-    small[0].start()
-    rowload.wait()
-    small[1].start()
+    copies = [pltpu.make_async_copy(new, new_hbm, ssem.at[0]), pltpu.make_async_copy(row, out_hbm, ssem.at[1])]
+    for c in copies:
+        c.start()
     for i in range(CHUNKS):
         @pl.loop(i * per, (i + 1) * per)
         def _(s):
@@ -390,31 +374,29 @@
                 kbuf[s, slot] = new[s, 0]
                 vbuf[s, slot] = new[s, 1]
 
-        for c in copies(i):
+        rows = pl.ds(i * per, per)
+        both = [pltpu.make_async_copy(kbuf.at[rows], ko_hbm.at[rows], osem.at[0, i]),
+                pltpu.make_async_copy(vbuf.at[rows], vo_hbm.at[rows], osem.at[1, i])]
+        for c in both:
             c.start()
-    for c in small:
+        copies += both
+    for c in copies:
         c.wait()
-    for i in range(CHUNKS):
-        for c in copies(i):
-            c.wait()
-
-
-def cache_call(*args):
+
+
+def cache_call(positions, new, row, k_loc, v_loc):
     hbm = pl.BlockSpec(memory_space=pl.ANY)
-    shape = (SEQS, SLOTS, KV_HEADS, HEAD_DIM)
-    new = (SEQS, 2, KV_HEADS, HEAD_DIM)
+    vm = pl.BlockSpec(memory_space=pltpu.VMEM)
     dma = pltpu.SemaphoreType.DMA
     return pl.pallas_call(
         cache_kernel,
         name="cache_write",
-        out_shape=(jax.ShapeDtypeStruct(shape, BF16), jax.ShapeDtypeStruct(shape, BF16), jax.ShapeDtypeStruct(new, BF16),
-                   jax.ShapeDtypeStruct((SEQS, DIM), BF16)),
-        in_specs=[pl.BlockSpec(memory_space=pltpu.SMEM)] + [hbm] * 2 + [pl.BlockSpec(memory_space=pltpu.VMEM)] * 2,
+        out_shape=tuple(jax.ShapeDtypeStruct(a.shape, a.dtype) for a in (k_loc, v_loc, new, row)),
+        in_specs=[pl.BlockSpec(memory_space=pltpu.SMEM)] + [vm] * 4,
+        out_specs=(hbm,) * 4,
+        scratch_shapes=[dma((2, CHUNKS)), dma((2,))],
         compiler_params=pltpu.CompilerParams(vmem_limit_bytes=12 * 2 ** 20),
-        out_specs=(hbm,) * 4,
-        scratch_shapes=[pltpu.VMEM((2, SEQS, 8, HEAD_DIM), F32), pltpu.VMEM(new, BF16), pltpu.VMEM((SEQS, DIM), BF16),
-                        dma((2, CHUNKS)), dma((4,))],
-    )(*args)
+    )(positions, new, row, k_loc, v_loc)
 
 
 def solution(mesh):
@@ -424,9 +406,9 @@
         inv = np.float32(ROPE_THETA) ** (-np.arange(HEAD_DIM // 2, dtype=np.float32) * np.float32(2.0) / np.float32(HEAD_DIM))
         freq = jnp.asarray(np.concatenate([inv, inv])[None, :].astype(np.float32))
         flat = (SEQS, SLOTS * KV_HEADS, HEAD_DIM)
-        row, kv, k_loc, v_loc = step_call(positions, tokens, attn_norm, q_norm[None, :], k_norm[None, :], freq, w_q, w_k, w_v,
-                                  w_o, k_cache.reshape(flat), v_cache.reshape(flat))
-        k_out, v_out, new_kv, block_out = cache_call(positions, kv, row, k_loc.reshape(k_cache.shape), v_loc.reshape(v_cache.shape))
+        operands = (positions, tokens, attn_norm, q_norm[None, :], k_norm[None, :], freq, w_q, w_k, w_v, w_o, k_cache.reshape(flat), v_cache.reshape(flat))
+        row, new, k_loc, v_loc = step_call(*[pltpu.with_memory_space_constraint(a, pltpu.HBM) for a in operands])
+        k_out, v_out, new_kv, block_out = cache_call(positions, new, row, k_loc.reshape(k_cache.shape), v_loc.reshape(v_cache.shape))
         return block_out, k_out, v_out, new_kv
 
     return jax.shard_map(device_step, mesh=mesh, in_specs=(P('dp', None), P('dp'), cache_spec, cache_spec, P(), P(), P(), P(), P(), P(), P()), out_specs=(P('dp', None), cache_spec, cache_spec, P('dp', None, None, None)), check_vma=False)

time: 53.6 us -> 48.1 us (0.90)
  local copies, waits for them, and re-layouts: 4.28 us -> 0.01 us
  Pallas kernels: 48.5 us -> 47.3 us
    unnamed x12 -> x2, local copies, waits for them, and re-layouts: 4.28 us -> 0.01 us
    pallas_call x1, Pallas kernels: 45.4 us -> 44.4 us  [step_call(): pl.pallas_call(step_kernel, name='decode_step', out_shape=(jax.ShapeDtype...]
where the time goes in v4:
time: 48.1 us; the launch traced here: 48 us
  Pallas kernels  47.3 us (98%)
  between operations  0.66 us (1%)
    pallas_call x1, Pallas kernels, step_call(): pl.pallas_call(step_kernel, name='decode_step', out_shape=(jax.ShapeDtype...  44.4 us
    pallas_call x1, Pallas kernels, cache_call(): pl.pallas_call(cache_kernel, name='cache_write', out_shape=tuple((jax.Sha...  2.88 us

profile of v4, /device:TPU:1, one launch (start us, length us, event | category | flops | bytes accessed | tf_op | source)
XLA Modules:
  0.0 48.0 jit_solution(7515724680391584175)
XLA Ops:
  0.6 0.0 copy-start
  0.6 44.4 %decode_step.1 = (bf16[64,2560]{1,0:T(8,128)(2,1)S(1)}, bf16[64,2,8,128]{3,2,1,0:T(8,128)(2,1)S(1)}, bf16[64,128,128]{2,1,0:T(8,128)(2,1)S(1)}, bf16[64,128,128]{2,1,0:T(8,128)(2,1)S(1)}) custom-call(s32[64]{0:T(128)} %pos_ref.1, bf16[64,2560]{1,0:T(8,128)(2,1)} %tok_hbm.1, bf16[2560]{0:T(1024)(128)(2,1)} %an_hbm.1, bf16[1,128]{1,0:T(2,128)(2,1)} %bitcast.10, ...), custom_call_target="tpu_custom_call" | custom-call | tf_op jit(solution)/shard_map/decode_step/pallas_call | solution.py:332
  45.1 0.0 copy-done
  45.1 2.9 %cache_write.1 = (bf16[64,16,8,128]{3,2,1,0:T(8,128)(2,1)}, bf16[64,16,8,128]{3,2,1,0:T(8,128)(2,1)}, bf16[64,2,8,128]{3,2,1,0:T(8,128)(2,1)}, bf16[64,2560]{1,0:T(8,128)(2,1)}) custom-call(s32[64]{0:T(128)S(1)} %copy-done, bf16[64,2,8,128]{3,2,1,0:T(8,128)(2,1)S(1)} %get-tuple-element.12.new, bf16[64,2560]{1,0:T(8,128)(2,1)S(1)} %get-tuple-element.13.row, ...), custom_call_target="tpu_custom_call" | custom-call | tf_op jit(solution)/shard_map/cache_write/pallas_call | solution.py:391
Async XLA Ops:
  0.6 44.4 %copy-start = (s32[64]{0:T(128)S(1)}, s32[64]{0:T(128)}, u32[]{:S(2)}) copy-start(s32[64]{0:T(128)} %pos_ref.1) | copy-start | bytes 772

commit v5 on v4

--- a/solution.py
+++ b/solution.py
@@ -18,6 +18,7 @@
 F32, BF16 = jnp.float32, jnp.bfloat16
 MESH = pl.DeviceIdType.MESH
 DEPTH = 3
+FAR_FIRST = sorted(range(16), key=lambda k: -(min(k // 4, 4 - k // 4) + min(k % 4, 4 - k % 4)))
 LAG = 5
 
 
@@ -42,7 +43,7 @@
                 ssend, srecv, tsend, trecv, ysem, bsend, brecv, fsend, frecv):
     me = lax.axis_index("sp")
     chip, core = me // 2, me % 2
-    zed = chip // 16
+    zed, low = lax.div(chip, 16), lax.rem(chip, 16)
     mate = chip * 2 + (1 - core)
     start = me * SLOTS
 
@@ -78,6 +79,13 @@
         c.start()
     for t in range(DEPTH):
         tile_copy(t).start()
+    def each_other(send):
+        for dz in (2, 1, 3, 0):
+            base = lax.rem(zed + dz, 4) * 16
+            for k in FAR_FIRST:
+                if dz or k:
+                    send(base + lax.rem(low + k, 16), (4 - dz) % 4)
+
     barrier = pltpu.get_barrier_semaphore()
     pl.semaphore_signal(barrier, inc=1, device_id=dev(mate), device_id_type=MESH)
 
@@ -188,12 +196,13 @@
             s = blk * 8 + s8
             here = lane16 == s8 * HALF + row16
             osend[s] = obuf[core, s] * pick(f0, here) + oin[s] * pick(f1, here)
+        group = lax.rem(zed - lax.div(blk, 2) + 4, 4)
         for s8 in range(8):
             s = blk * 8 + s8
 
             @pl.when(s != chip)
             def _():
-                pltpu.make_async_remote_copy(src_ref=osend.at[s], dst_ref=rbuf.at[chip], send_sem=ssend.at[0], recv_sem=srecv.at[lax.rem(zed - s // 16 + 4, 4)],
+                pltpu.make_async_remote_copy(src_ref=osend.at[s], dst_ref=rbuf.at[chip], send_sem=ssend.at[0], recv_sem=srecv.at[group],
                                              device_id=dev(s * 2 + core), device_id_type=MESH).start()
 
     @pl.loop(0, 8)
@@ -216,11 +225,11 @@
     stsend[:, 0, :] = top
     stsend[:, 1, :] = l0 * f0 + l1 * f1
 
-    @pl.loop(1, CHIPS)
-    def _(off):
-        s = lax.rem(chip + off, CHIPS)
-        pltpu.make_async_remote_copy(src_ref=stsend.at[s // 8], dst_ref=rst.at[chip], send_sem=tsend.at[0], recv_sem=trecv.at[0],
+    def send_stats(s, _):
+        pltpu.make_async_remote_copy(src_ref=stsend.at[lax.div(s, 8)], dst_ref=rst.at[chip], send_sem=tsend.at[0], recv_sem=trecv.at[0],
                                      device_id=dev(s * 2 + core), device_id_type=MESH).start()
+
+    each_other(send_stats)
 
     @pl.loop(LAG, 8 + LAG)
     def _(i):
@@ -237,9 +246,22 @@
         return pltpu.make_async_remote_copy(src_ref=src, dst_ref=dst, send_sem=send, recv_sem=recv, device_id=dev(mate),
                                             device_id_type=MESH)
 
-    low = iota((SEQS, 8, HEAD_DIM), 1) < 4
-    new_ref[:, 0] = jnp.where(low, gbuf[4], pltpu.roll(gbuf[5], 4, 1)).astype(BF16)
-    new_ref[:, 1] = jnp.where(low, pltpu.roll(gbuf[4], 4, 1), gbuf[5]).astype(BF16)
+    upper = iota((SEQS, 8, HEAD_DIM), 1) < 4
+    new_ref[:, 0] = jnp.where(upper, gbuf[4], pltpu.roll(gbuf[5], 4, 1)).astype(BF16)
+    new_ref[:, 1] = jnp.where(upper, pltpu.roll(gbuf[4], 4, 1), gbuf[5]).astype(BF16)
+
+    slot_row = iota((128, HEAD_DIM), 0) // KV_HEADS + start
+
+    @pl.loop(0, 16)
+    def _(i):
+        for s4 in range(4):
+            s = i * 4 + s4
+            first, second = gbuf[4, s], gbuf[5, s]
+            mine = slot_row == pos_ref[s]
+            k_new = jnp.where(upper[0], first, pltpu.roll(second, 4, 0))
+            v_new = jnp.where(upper[0], pltpu.roll(first, 4, 0), second)
+            kbuf[s] = jnp.where(mine, jnp.concatenate([k_new] * SLOTS, axis=0).astype(BF16), kbuf[s])
+            vbuf[s] = jnp.where(mine, jnp.concatenate([v_new] * SLOTS, axis=0).astype(BF16), vbuf[s])
 
     others = pl.ds(0, CHIPS - 1)
     all_of(rst.at[others], rst.at[others], tsend.at[0], trecv.at[0]).wait_recv()
@@ -290,10 +312,7 @@
         return pltpu.make_async_remote_copy(src_ref=ysend, dst_ref=ybuf.at[core, chip], send_sem=bsend.at[0],
                                             recv_sem=brecv.at[group], device_id=dev(s * 2 + core), device_id_type=MESH)
 
-    @pl.loop(1, CHIPS)
-    def _(k):
-        s = lax.rem(chip + 1 + lax.rem(k + 30, CHIPS - 1), CHIPS)
-        bcopy(s, lax.rem(zed - s // 16 + 4, 4)).start()
+    each_other(lambda s, group: bcopy(s, group).start())
 
     ybuf[core, chip] = ysend[...]
 
@@ -305,17 +324,20 @@
         return pltpu.make_async_remote_copy(src_ref=ref, dst_ref=ref, send_sem=fsend.at[group], recv_sem=frecv.at[group],
                                             device_id=dev(mate), device_id_type=MESH)
 
+    def finish(half, group):
+        rows = pl.ds(pl.multiple_of(lax.rem(zed + group, 4) * 16, 16), 16)
+        for k in range(10):
+            cols = pl.ds(pl.multiple_of(half * 1280 + k * 128, 128), 128)
+            out_ref[rows, cols] = (tok_ref[rows, cols].astype(F32) + ybuf[half, rows, k, :]).astype(BF16)
+
     for group in (0, 1, 3, 2):
         ref = ybuf.at[core, pl.ds(0, 15 if group == 0 else 16)]
         all_of(ref, ref, bsend.at[0], brecv.at[group]).wait_recv()
         fcopy(core, group).start()
+        finish(core, group)
     for group in (0, 1, 3, 2):
         fcopy(1 - core, group).wait_recv()
-
-    for half in range(2):
-        for k in range(10):
-            cols = slice(half * 1280 + k * 128, half * 1280 + (k + 1) * 128)
-            out_ref[:, cols] = (tok_ref[:, cols].astype(F32) + ybuf[half, :, k, :]).astype(BF16)
+        finish(1 - core, group)
 
     for group in range(4):
         fcopy(core, group).wait_send()
@@ -355,48 +377,26 @@
     )(*args)
 
 
-CHUNKS = 8
-
-
-def cache_kernel(pos_ref, new, row, kbuf, vbuf, ko_hbm, vo_hbm, new_hbm, out_hbm, osem, ssem):
-    start = lax.axis_index("sp") * SLOTS
-    per = SEQS // CHUNKS
-    copies = [pltpu.make_async_copy(new, new_hbm, ssem.at[0]), pltpu.make_async_copy(row, out_hbm, ssem.at[1])]
+def store_kernel(*refs):
+    sem = refs[-1]
+    count = (len(refs) - 1) // 2
+    copies = [pltpu.make_async_copy(refs[i], refs[count + i], sem.at[i]) for i in range(count)]
     for c in copies:
         c.start()
-    for i in range(CHUNKS):
-        @pl.loop(i * per, (i + 1) * per)
-        def _(s):
-            slot = pos_ref[s] - start
-
-            @pl.when((slot >= 0) & (slot < SLOTS))
-            def _():
-                kbuf[s, slot] = new[s, 0]
-                vbuf[s, slot] = new[s, 1]
-
-        rows = pl.ds(i * per, per)
-        both = [pltpu.make_async_copy(kbuf.at[rows], ko_hbm.at[rows], osem.at[0, i]),
-                pltpu.make_async_copy(vbuf.at[rows], vo_hbm.at[rows], osem.at[1, i])]
-        for c in both:
-            c.start()
-        copies += both
     for c in copies:
         c.wait()
 
 
-def cache_call(positions, new, row, k_loc, v_loc):
-    hbm = pl.BlockSpec(memory_space=pl.ANY)
-    vm = pl.BlockSpec(memory_space=pltpu.VMEM)
-    dma = pltpu.SemaphoreType.DMA
+def store_call(*arrays):
     return pl.pallas_call(
-        cache_kernel,
-        name="cache_write",
-        out_shape=tuple(jax.ShapeDtypeStruct(a.shape, a.dtype) for a in (k_loc, v_loc, new, row)),
-        in_specs=[pl.BlockSpec(memory_space=pltpu.SMEM)] + [vm] * 4,
-        out_specs=(hbm,) * 4,
-        scratch_shapes=[dma((2, CHUNKS)), dma((2,))],
+        store_kernel,
+        name="store",
+        out_shape=tuple(jax.ShapeDtypeStruct(a.shape, a.dtype) for a in arrays),
+        in_specs=[pl.BlockSpec(memory_space=pltpu.VMEM)] * len(arrays),
+        out_specs=(pl.BlockSpec(memory_space=pl.ANY),) * len(arrays),
+        scratch_shapes=[pltpu.SemaphoreType.DMA((len(arrays),))],
         compiler_params=pltpu.CompilerParams(vmem_limit_bytes=12 * 2 ** 20),
-    )(positions, new, row, k_loc, v_loc)
+    )(*arrays)
 
 
 def solution(mesh):
@@ -408,7 +408,7 @@
         flat = (SEQS, SLOTS * KV_HEADS, HEAD_DIM)
         operands = (positions, tokens, attn_norm, q_norm[None, :], k_norm[None, :], freq, w_q, w_k, w_v, w_o, k_cache.reshape(flat), v_cache.reshape(flat))
         row, new, k_loc, v_loc = step_call(*[pltpu.with_memory_space_constraint(a, pltpu.HBM) for a in operands])
-        k_out, v_out, new_kv, block_out = cache_call(positions, new, row, k_loc.reshape(k_cache.shape), v_loc.reshape(v_cache.shape))
+        k_out, v_out, new_kv, block_out = store_call(k_loc.reshape(k_cache.shape), v_loc.reshape(v_cache.shape), new, row)
         return block_out, k_out, v_out, new_kv
 
     return jax.shard_map(device_step, mesh=mesh, in_specs=(P('dp', None), P('dp'), cache_spec, cache_spec, P(), P(), P(), P(), P(), P(), P()), out_specs=(P('dp', None), cache_spec, cache_spec, P('dp', None, None, None)), check_vma=False)

time: 48.1 us -> 45.9 us (0.954)
  Pallas kernels: 47.3 us -> 45.1 us
    pallas_call x1, Pallas kernels: 44.4 us -> 42.9 us  [step_call(): pl.pallas_call(step_kernel, name='decode_step', out_shape=(jax.ShapeDtype...]
    pallas_call x1, Pallas kernels: 2.88 us -> 2.22 us  [store_call(): pl.pallas_call(store_kernel, name='store', out_shape=tuple((jax.ShapeDtyp...]
where the time goes in v5:
time: 45.9 us; the launch traced here: 45.7 us
  Pallas kernels  45.1 us (98%)
  between operations  0.64 us (1%)
    pallas_call x1, Pallas kernels, step_call(): pl.pallas_call(step_kernel, name='decode_step', out_shape=(jax.ShapeDtype...  42.9 us
    pallas_call x1, Pallas kernels, store_call(): pl.pallas_call(store_kernel, name='store', out_shape=tuple((jax.ShapeDtyp...  2.22 us

profile of v5, /device:TPU:1, one launch (start us, length us, event | category | flops | bytes accessed | tf_op | source)
XLA Modules:
  0.0 45.7 jit_solution(14779900910638632775)
XLA Ops:
  0.6 42.9 %decode_step.1 = (bf16[64,2560]{1,0:T(8,128)(2,1)S(1)}, bf16[64,2,8,128]{3,2,1,0:T(8,128)(2,1)S(1)}, bf16[64,128,128]{2,1,0:T(8,128)(2,1)S(1)}, bf16[64,128,128]{2,1,0:T(8,128)(2,1)S(1)}) custom-call(s32[64]{0:T(128)} %pos_hbm.1, bf16[64,2560]{1,0:T(8,128)(2,1)} %tok_hbm.1, bf16[2560]{0:T(1024)(128)(2,1)} %an_hbm.1, bf16[1,128]{1,0:T(2,128)(2,1)} %bitcast.10, ...), custom_call_target="tpu_custom_call" | custom-call | tf_op jit(solution)/shard_map/decode_step/pallas_call | solution.py:354
  43.5 2.2 %store.1 = (bf16[64,16,8,128]{3,2,1,0:T(8,128)(2,1)}, bf16[64,16,8,128]{3,2,1,0:T(8,128)(2,1)}, bf16[64,2,8,128]{3,2,1,0:T(8,128)(2,1)}, bf16[64,2560]{1,0:T(8,128)(2,1)}) custom-call(bf16[64,16,8,128]{3,2,1,0:T(8,128)(2,1)S(1)} %bitcast.6, bf16[64,16,8,128]{3,2,1,0:T(8,128)(2,1)S(1)} %bitcast.7, bf16[64,2,8,128]{3,2,1,0:T(8,128)(2,1)S(1)} %get-tuple-element.14.refs_2_, ...), custom_call_target="tpu_custom_call" | custom-call | tf_op jit(solution)/shard_map/store/pallas_call | solution.py:391

commit v6 on v5

--- a/solution.py
+++ b/solution.py
@@ -17,7 +17,8 @@
 SCALE = HEAD_DIM ** -0.5
 F32, BF16 = jnp.float32, jnp.bfloat16
 MESH = pl.DeviceIdType.MESH
-DEPTH = 3
+DEPTH = 2
+TILES = 6
 FAR_FIRST = sorted(range(16), key=lambda k: -(min(k // 4, 4 - k // 4) + min(k % 4, 4 - k % 4)))
 LAG = 5
 
@@ -50,15 +51,10 @@
     def dev(index):
         return (lax.axis_index("dp"), index)
 
-    def wcopy(src, col, tile):
-        return pltpu.make_async_copy(src.at[:, pl.ds(pl.multiple_of(col, 256), 256)], wbuf.at[tile], wsem.at[tile])
-
     def tile_copy(t):
-        if t < 2:
-            return wcopy(wk_hbm, core * 512 + t * 256, t)
-        if t < 4:
-            return wcopy(wv_hbm, core * 512 + (t - 2) * 256, t)
-        return wcopy(wq_hbm, core * 2048 + (t - 4) * 256, t)
+        src, col = ((wk_hbm, 0), (wv_hbm, 0))[t] if t < 2 else (wq_hbm, (t - 2) * 512)
+        col = pl.multiple_of(core * (512 if t < 2 else 2048) + col, 512)
+        return pltpu.make_async_copy(src.at[:, pl.ds(col, 512)], wbuf.at[t], wsem.at[t])
 
     def kvload(i):
         rows = pl.ds(i * 16, 16)
@@ -67,11 +63,12 @@
 
     def tile_ready(t):
         tile_copy(t).wait()
-        if t + DEPTH < 12:
+        if t + DEPTH < TILES:
             tile_copy(t + DEPTH).start()
-        elif t + DEPTH < 14:
-            for c in kvload(2 * (t + DEPTH - 12)) + kvload(2 * (t + DEPTH - 12) + 1):
-                c.start()
+        else:
+            for i in (2 * (t + DEPTH - TILES), 2 * (t + DEPTH - TILES) + 1):
+                for c in kvload(i):
+                    c.start()
 
     inputs = [pltpu.make_async_copy(a, b, isem.at[i]) for i, (a, b) in enumerate(
         [(tok_hbm, tok_ref), (an_hbm, an_ref), (pos_hbm, pos_ref), (freq_hbm, freq_ref), (kn_hbm, kn_ref), (qn_hbm, qn_ref)])]
@@ -114,24 +111,24 @@
         turned = normed * cosr[...] + pltpu.roll(normed, HEAD_DIM // 2, 1) * sinr[...]
         return turned.astype(BF16).astype(F32)
 
-    for t in range(4):
+    for t in range(2):
         tile_ready(t)
         res = project(t)
-        for h in range(2):
+        for h in range(4):
             head = res[:, h * 128:(h + 1) * 128]
-            gbuf[4 + core, :, 2 * t + h, :] = rope(head, kn_ref[...].astype(F32)) if t < 2 else head
+            gbuf[4 + core, :, 4 * t + h, :] = head if t else rope(head, kn_ref[...].astype(F32))
 
     def gcopy(group, slot):
         return pltpu.make_async_remote_copy(src_ref=gbuf.at[group], dst_ref=gbuf.at[group], send_sem=gsend.at[slot],
                                             recv_sem=grecv.at[slot], device_id=dev(mate), device_id_type=MESH)
 
     for g in range(2):
-        for t4 in range(4):
-            t = 4 + g * 4 + t4
+        for t2 in range(2):
+            t = 2 + g * 2 + t2
             tile_ready(t)
             res = project(t)
-            for h in range(2):
-                gbuf[2 * core + g, :, 2 * t4 + h, :] = rope(res[:, h * 128:(h + 1) * 128], qn_ref[...].astype(F32))
+            for h in range(4):
+                gbuf[2 * core + g, :, 4 * t2 + h, :] = rope(res[:, h * 128:(h + 1) * 128], qn_ref[...].astype(F32))
         if g == 0:
             pl.semaphore_wait(barrier, CHIPS)
             gcopy(4 + core, 2).start()
@@ -293,12 +290,10 @@
     wocopy.wait()
 
     def out_cols(half, slot):
-        for n in range(5):
-            cols = pl.ds(pl.multiple_of(half * 1280 + n * 256, 256), 256)
-            res = jnp.dot(lhs[...], wobuf[:, cols], preferred_element_type=F32)
-            res = jnp.sum(res, axis=0, keepdims=True)
-            for k in range(2):
-                ypart[slot, pl.ds(2 * n + k, 1), :] = res[:, k * 128:(k + 1) * 128]
+        cols = pl.ds(pl.multiple_of(half * 1280, 1280), 1280)
+        res = jnp.sum(jnp.dot(lhs[...], wobuf[:, cols], preferred_element_type=F32), axis=0, keepdims=True)
+        for k in range(10):
+            ypart[slot, pl.ds(k, 1), :] = res[:, k * 128:(k + 1) * 128]
 
     out_cols(1 - core, 0)
     ycopy = pltpu.make_async_remote_copy(src_ref=ypart.at[0], dst_ref=yin, send_sem=ysem.at[0], recv_sem=ysem.at[1],
@@ -362,7 +357,7 @@
             pltpu.SMEM((SEQS,), jnp.int32), vmem((SEQS, DIM), BF16), vmem((DIM,), BF16), vmem((1, HEAD_DIM), BF16), vmem((1, HEAD_DIM), BF16), vmem((1, HEAD_DIM), F32),
             dma((6,)), vmem((CHIPS, HEAD_DIM), F32),
             vmem((SEQS, DIM), BF16), vmem((SEQS, HEAD_DIM), F32), vmem((SEQS, HEAD_DIM), F32),
-            vmem((12, DIM, 256), BF16), vmem((2048, DIM), BF16),
+            vmem((TILES, DIM, 512), BF16), vmem((2048, DIM), BF16),
             vmem((6, SEQS, 8, HEAD_DIM), F32),
             vmem((SEQS, HEADS, HEAD_DIM), BF16), vmem((2, SEQS, HALF, HEAD_DIM), F32), vmem((SEQS, HALF, HEAD_DIM), F32),
             vmem((2, 8, 2, HEAD_DIM), F32), vmem((8, 2, HEAD_DIM), F32), vmem((2, 8, HEAD_DIM), F32),
@@ -370,7 +365,7 @@
             vmem((CHIPS, HALF, HEAD_DIM), F32), vmem((CHIPS, 2, HEAD_DIM), F32),
             vmem((HALF, 2048), BF16), vmem((2, 10, HEAD_DIM), F32), vmem((10, HEAD_DIM), F32), vmem((10, HEAD_DIM), F32),
             vmem((2, CHIPS, 10, HEAD_DIM), F32),
-            dma((12,)), dma((1,)), dma((2, 4)), dma((3,)), dma((3,)), dma((8,)), dma((8,)), dma((1,)), dma((1,)),
+            dma((TILES,)), dma((1,)), dma((2, 4)), dma((3,)), dma((3,)), dma((8,)), dma((8,)), dma((1,)), dma((1,)),
             dma((1,)), dma((4,)), dma((1,)), dma((1,)), dma((2,)), dma((1,)), dma((4,)), dma((4,)), dma((4,)),
         ],
         compiler_params=pltpu.CompilerParams(collective_id=0, has_side_effects=True, vmem_limit_bytes=48 * 2 ** 20),

time: 45.9 us -> 43.3 us (0.943)
  Pallas kernels: 45.1 us -> 42.6 us
    pallas_call x1, Pallas kernels: 42.9 us -> 40.4 us  [step_call(): pl.pallas_call(step_kernel, name='decode_step', out_shape=(jax.ShapeDtype...]
where the time goes in v6:
time: 43.3 us; the launch traced here: 43.2 us
  Pallas kernels  42.6 us (98%)
  between operations  0.64 us (1%)
    pallas_call x1, Pallas kernels, step_call(): pl.pallas_call(step_kernel, name='decode_step', out_shape=(jax.ShapeDtype...  40.4 us
    pallas_call x1, Pallas kernels, store_call(): pl.pallas_call(store_kernel, name='store', out_shape=tuple((jax.ShapeDtyp...  2.22 us

profile of v6, /device:TPU:1, one launch (start us, length us, event | category | flops | bytes accessed | tf_op | source)
XLA Modules:
  0.0 43.2 jit_solution(7745772339367285359)
XLA Ops:
  0.6 40.4 %decode_step.1 = (bf16[64,2560]{1,0:T(8,128)(2,1)S(1)}, bf16[64,2,8,128]{3,2,1,0:T(8,128)(2,1)S(1)}, bf16[64,128,128]{2,1,0:T(8,128)(2,1)S(1)}, bf16[64,128,128]{2,1,0:T(8,128)(2,1)S(1)}) custom-call(s32[64]{0:T(128)} %pos_hbm.1, bf16[64,2560]{1,0:T(8,128)(2,1)} %tok_hbm.1, bf16[2560]{0:T(1024)(128)(2,1)} %an_hbm.1, bf16[1,128]{1,0:T(2,128)(2,1)} %bitcast.10, ...), custom_call_target="tpu_custom_call" | custom-call | tf_op jit(solution)/shard_map/decode_step/pallas_call | solution.py:349
  41.0 2.2 %store.1 = (bf16[64,16,8,128]{3,2,1,0:T(8,128)(2,1)}, bf16[64,16,8,128]{3,2,1,0:T(8,128)(2,1)}, bf16[64,2,8,128]{3,2,1,0:T(8,128)(2,1)}, bf16[64,2560]{1,0:T(8,128)(2,1)}) custom-call(bf16[64,16,8,128]{3,2,1,0:T(8,128)(2,1)S(1)} %bitcast.6, bf16[64,16,8,128]{3,2,1,0:T(8,128)(2,1)S(1)} %bitcast.7, bf16[64,2,8,128]{3,2,1,0:T(8,128)(2,1)S(1)} %get-tuple-element.14.refs_2_, ...), custom_call_target="tpu_custom_call" | custom-call | tf_op jit(solution)/shard_map/store/pallas_call | solution.py:386

commit v7 on v6

--- a/solution.py
+++ b/solution.py
@@ -19,7 +19,8 @@
 MESH = pl.DeviceIdType.MESH
 DEPTH = 2
 TILES = 6
-FAR_FIRST = sorted(range(16), key=lambda k: -(min(k // 4, 4 - k // 4) + min(k % 4, 4 - k % 4)))
+HOPS = (0, 1, 2, 1)
+OFFSETS = sorted(((a, b, c) for a in range(4) for b in range(4) for c in range(4)), key=lambda o: -sum(HOPS[d] for d in o))
 LAG = 5
 
 
@@ -44,7 +45,12 @@
                 ssend, srecv, tsend, trecv, ysem, bsend, brecv, fsend, frecv):
     me = lax.axis_index("sp")
     chip, core = me // 2, me % 2
-    zed, low = lax.div(chip, 16), lax.rem(chip, 16)
+    place = (lax.div(chip, 16), lax.rem(lax.div(chip, 4), 4), lax.rem(chip, 4))
+    zed = place[0]
+    turn = [[lax.rem(p + d, 4) * w for d in range(4)] for p, w in zip(place, (16, 4, 1))]
+
+    def chip_at(offset):
+        return turn[0][offset[0]] + turn[1][offset[1]] + turn[2][offset[2]]
     mate = chip * 2 + (1 - core)
     start = me * SLOTS
 
@@ -77,11 +83,8 @@
     for t in range(DEPTH):
         tile_copy(t).start()
     def each_other(send):
-        for dz in (2, 1, 3, 0):
-            base = lax.rem(zed + dz, 4) * 16
-            for k in FAR_FIRST:
-                if dz or k:
-                    send(base + lax.rem(low + k, 16), (4 - dz) % 4)
+        for o in OFFSETS[:-1]:
+            send(chip_at(o), (4 - o[0]) % 4)
 
     barrier = pltpu.get_barrier_semaphore()
     pl.semaphore_signal(barrier, inc=1, device_id=dev(mate), device_id_type=MESH)
@@ -141,9 +144,6 @@
     for i in range(4):
         for c in kvload(i):
             c.wait()
-
-    def block_of(i):
-        return lax.rem(zed + 2 + i // 2 - (i // 4) * (2 * (i // 2) - 1), 4) * 2 + lax.rem(i, 2)
 
     row32, col32 = iota((HEADS, HEAD_DIM), 0), iota((HEADS, HEAD_DIM), 1)
     same_head = (col32 % KV_HEADS) == (row32 // 4)
@@ -172,35 +172,29 @@
                 st[half, blk, pl.ds(k, 1), :] = jnp.sum(acc[half][k], axis=0, keepdims=True)
 
     def mix(i):
-        blk = block_of(i)
-        for s8 in range(8):
-            s = blk * 8 + s8
+        for n in range(8 * i, 8 * i + 8):
+            s = chip_at(OFFSETS[n])
             mixed = jnp.dot(wts[s], vbuf[s], preferred_element_type=F32)
             for half in range(2):
-                obuf[half, s] = mixed[half * HALF:(half + 1) * HALF]
+                obuf[half, n] = mixed[half * HALF:(half + 1) * HALF]
         ocopy(i).start()
 
     def ocopy(i):
-        rows = pl.ds(block_of(i) * 8, 8)
+        rows = pl.ds(i * 8, 8)
         return pltpu.make_async_remote_copy(src_ref=obuf.at[1 - core, rows], dst_ref=oin.at[rows], send_sem=dsend.at[i],
                                             recv_sem=drecv.at[i], device_id=dev(mate), device_id_type=MESH)
 
     def merge(i):
-        blk = block_of(i)
         ocopy(i).wait()
-        f0, f1 = fac[0, pl.ds(blk, 1), :], fac[1, pl.ds(blk, 1), :]
-        for s8 in range(8):
-            s = blk * 8 + s8
-            here = lane16 == s8 * HALF + row16
-            osend[s] = obuf[core, s] * pick(f0, here) + oin[s] * pick(f1, here)
-        group = lax.rem(zed - lax.div(blk, 2) + 4, 4)
-        for s8 in range(8):
-            s = blk * 8 + s8
-
-            @pl.when(s != chip)
-            def _():
-                pltpu.make_async_remote_copy(src_ref=osend.at[s], dst_ref=rbuf.at[chip], send_sem=ssend.at[0], recv_sem=srecv.at[group],
-                                             device_id=dev(s * 2 + core), device_id_type=MESH).start()
+        for n in range(8 * i, 8 * i + 8):
+            s = chip_at(OFFSETS[n])
+            here = lane16 == lax.rem(s, 8) * HALF + row16
+            f0, f1 = fac[0, pl.ds(lax.div(s, 8), 1), :], fac[1, pl.ds(lax.div(s, 8), 1), :]
+            osend[n] = obuf[core, n] * pick(f0, here) + oin[n] * pick(f1, here)
+        for n in range(8 * i, min(8 * i + 8, CHIPS - 1)):
+            pltpu.make_async_remote_copy(src_ref=osend.at[n], dst_ref=rbuf.at[chip], send_sem=ssend.at[0],
+                                         recv_sem=srecv.at[(4 - OFFSETS[n][0]) % 4],
+                                         device_id=dev(chip_at(OFFSETS[n]) * 2 + core), device_id_type=MESH).start()
 
     @pl.loop(0, 8)
     def _(blk):
@@ -210,8 +204,7 @@
                                           device_id=dev(mate), device_id_type=MESH)
     stcopy.start()
 
-    @pl.loop(0, LAG)
-    def _(i):
+    for i in range(LAG):
         mix(i)
 
     stcopy.wait()
@@ -228,16 +221,13 @@
 
     each_other(send_stats)
 
-    @pl.loop(LAG, 8 + LAG)
-    def _(i):
-        @pl.when(i < 8)
-        def _():
+    for i in range(LAG, 8 + LAG):
+        if i < 8:
             mix(i)
-
         merge(i - LAG)
 
     rst[chip] = stsend[chip // 8]
-    rbuf[chip] = osend[chip]
+    rbuf[chip] = osend[CHIPS - 1]
 
     def all_of(src, dst, send, recv):
         return pltpu.make_async_remote_copy(src_ref=src, dst_ref=dst, send_sem=send, recv_sem=recv, device_id=dev(mate),

time: 43.3 us -> 43.5 us (level)
  no operation moved by 1% of the time
where the time goes in v7:
time: 43.5 us; the launch traced here: 43.4 us
  Pallas kernels  42.7 us (98%)
  between operations  0.64 us (1%)
    pallas_call x1, Pallas kernels, step_call(): pl.pallas_call(step_kernel, name='decode_step', out_shape=(jax.ShapeDtype...  40.5 us
    pallas_call x1, Pallas kernels, store_call(): pl.pallas_call(store_kernel, name='store', out_shape=tuple((jax.ShapeDtyp...  2.22 us

profile of v7, /device:TPU:1, one launch (start us, length us, event | category | flops | bytes accessed | tf_op | source)
XLA Modules:
  0.0 43.4 jit_solution(16304746035203046745)
XLA Ops:
  0.6 40.5 %decode_step.1 = (bf16[64,2560]{1,0:T(8,128)(2,1)S(1)}, bf16[64,2,8,128]{3,2,1,0:T(8,128)(2,1)S(1)}, bf16[64,128,128]{2,1,0:T(8,128)(2,1)S(1)}, bf16[64,128,128]{2,1,0:T(8,128)(2,1)S(1)}) custom-call(s32[64]{0:T(128)} %pos_hbm.1, bf16[64,2560]{1,0:T(8,128)(2,1)} %tok_hbm.1, bf16[2560]{0:T(1024)(128)(2,1)} %an_hbm.1, bf16[1,128]{1,0:T(2,128)(2,1)} %bitcast.10, ...), custom_call_target="tpu_custom_call" | custom-call | tf_op jit(solution)/shard_map/decode_step/pallas_call | solution.py:339
  41.1 2.2 %store.1 = (bf16[64,16,8,128]{3,2,1,0:T(8,128)(2,1)}, bf16[64,16,8,128]{3,2,1,0:T(8,128)(2,1)}, bf16[64,2,8,128]{3,2,1,0:T(8,128)(2,1)}, bf16[64,2560]{1,0:T(8,128)(2,1)}) custom-call(bf16[64,16,8,128]{3,2,1,0:T(8,128)(2,1)S(1)} %bitcast.6, bf16[64,16,8,128]{3,2,1,0:T(8,128)(2,1)S(1)} %bitcast.7, bf16[64,2,8,128]{3,2,1,0:T(8,128)(2,1)S(1)} %get-tuple-element.14.refs_2_, ...), custom_call_target="tpu_custom_call" | custom-call | tf_op jit(solution)/shard_map/store/pallas_call | solution.py:376

commit v8 on v6

--- a/solution.py
+++ b/solution.py
@@ -90,6 +90,8 @@
     def _(off):
         pl.semaphore_signal(barrier, inc=1, device_id=dev(lax.rem(chip + off, CHIPS) * 2 + core), device_id_type=MESH)
 
+    for n in range(2):
+        wts[:, pl.ds(n * HEADS, HEADS), pl.ds((1 - n) * HEAD_DIM, HEAD_DIM)] = jnp.zeros((SEQS // 2, HEADS, HEAD_DIM), BF16)
     for c in inputs:
         c.wait()
 
@@ -152,32 +154,40 @@
 
     def weigh(blk):
         acc = [[jnp.zeros((HALF, HEAD_DIM), F32) for _ in range(2)] for _ in range(2)]
-        for s8 in range(8):
-            s = blk * 8 + s8
-            q = jnp.concatenate([gbuf[g, s] for g in range(4)], axis=0).astype(BF16)
-            scores = lax.dot_general(q, kbuf[s], (((1,), (1,)), ((), ())), preferred_element_type=F32) * SCALE
-            live = same_head & (slot_of < pos_ref[s])
-            scores = jnp.where(live, scores, NEG_FILL)
-            peak = jnp.max(scores, axis=-1, keepdims=True)
-            weights = jnp.where(live, jnp.exp(scores - peak), 0.0)
-            total = jnp.sum(weights, axis=-1, keepdims=True)
-            wts[s] = weights.astype(BF16)
-            here = lane16 == s8 * HALF + row16
-            for half in range(2):
-                cut = slice(half * HALF, (half + 1) * HALF)
-                acc[half][0] += jnp.where(here, peak[cut], 0.0)
-                acc[half][1] += jnp.where(here, total[cut], 0.0)
+        for p4 in range(4):
+            pair = blk * 4 + p4
+            both = pl.ds(pair * 2, 2)
+            q = jnp.concatenate([gbuf[g, pair * 2 + n] for n in range(2) for g in range(4)], axis=0).astype(BF16)
+            keys = kbuf[both].reshape(2 * HEAD_DIM, HEAD_DIM)
+            products = lax.dot_general(q, keys, (((1,), (1,)), ((), ())), preferred_element_type=F32)
+            for n in range(2):
+                rows, cols = pl.ds(n * HEADS, HEADS), pl.ds(n * HEAD_DIM, HEAD_DIM)
+                scores = products[n * HEADS:(n + 1) * HEADS, n * HEAD_DIM:(n + 1) * HEAD_DIM] * SCALE
+                live = same_head & (slot_of < pos_ref[pair * 2 + n])
+                scores = jnp.where(live, scores, NEG_FILL)
+                peak = jnp.max(scores, axis=-1, keepdims=True)
+                weights = jnp.where(live, jnp.exp(scores - peak), 0.0)
+                total = jnp.sum(weights, axis=-1, keepdims=True)
+                wts[pair, rows, cols] = weights.astype(BF16)
+                here = lane16 == (p4 * 2 + n) * HALF + row16
+                for half in range(2):
+                    cut = slice(half * HALF, (half + 1) * HALF)
+                    acc[half][0] += jnp.where(here, peak[cut], 0.0)
+                    acc[half][1] += jnp.where(here, total[cut], 0.0)
         for half in range(2):
             for k in range(2):
                 st[half, blk, pl.ds(k, 1), :] = jnp.sum(acc[half][k], axis=0, keepdims=True)
 
     def mix(i):
         blk = block_of(i)
-        for s8 in range(8):
-            s = blk * 8 + s8
-            mixed = jnp.dot(wts[s], vbuf[s], preferred_element_type=F32)
-            for half in range(2):
-                obuf[half, s] = mixed[half * HALF:(half + 1) * HALF]
+        for p4 in range(4):
+            pair = blk * 4 + p4
+            values = vbuf[pl.ds(pair * 2, 2)].reshape(2 * HEAD_DIM, HEAD_DIM)
+            mixed = jnp.dot(wts[pair], values, preferred_element_type=F32)
+            for n in range(2):
+                for half in range(2):
+                    top = n * HEADS + half * HALF
+                    obuf[half, pair * 2 + n] = mixed[top:top + HALF]
         ocopy(i).start()
 
     def ocopy(i):
@@ -359,7 +369,7 @@
             vmem((SEQS, DIM), BF16), vmem((SEQS, HEAD_DIM), F32), vmem((SEQS, HEAD_DIM), F32),
             vmem((TILES, DIM, 512), BF16), vmem((2048, DIM), BF16),
             vmem((6, SEQS, 8, HEAD_DIM), F32),
-            vmem((SEQS, HEADS, HEAD_DIM), BF16), vmem((2, SEQS, HALF, HEAD_DIM), F32), vmem((SEQS, HALF, HEAD_DIM), F32),
+            vmem((SEQS // 2, 2 * HEADS, 2 * HEAD_DIM), BF16), vmem((2, SEQS, HALF, HEAD_DIM), F32), vmem((SEQS, HALF, HEAD_DIM), F32),
             vmem((2, 8, 2, HEAD_DIM), F32), vmem((8, 2, HEAD_DIM), F32), vmem((2, 8, HEAD_DIM), F32),
             vmem((SEQS, HALF, HEAD_DIM), F32), vmem((8, 2, HEAD_DIM), F32),
             vmem((CHIPS, HALF, HEAD_DIM), F32), vmem((CHIPS, 2, HEAD_DIM), F32),

time: 43.3 us -> 43 us (level)
  no operation moved by 1% of the time
where the time goes in v8:
time: 43 us; the launch traced here: 42.9 us
  Pallas kernels  42.2 us (98%)
  between operations  0.64 us (1%)
    pallas_call x1, Pallas kernels, step_call(): pl.pallas_call(step_kernel, name='decode_step', out_shape=(jax.ShapeDtype...  40 us
    pallas_call x1, Pallas kernels, store_call(): pl.pallas_call(store_kernel, name='store', out_shape=tuple((jax.ShapeDtyp...  2.22 us

profile of v8, /device:TPU:1, one launch (start us, length us, event | category | flops | bytes accessed | tf_op | source)
XLA Modules:
  0.0 42.9 jit_solution(1275701610212223454)
XLA Ops:
  0.6 40.0 %decode_step.1 = (bf16[64,2560]{1,0:T(8,128)(2,1)S(1)}, bf16[64,2,8,128]{3,2,1,0:T(8,128)(2,1)S(1)}, bf16[64,128,128]{2,1,0:T(8,128)(2,1)S(1)}, bf16[64,128,128]{2,1,0:T(8,128)(2,1)S(1)}) custom-call(s32[64]{0:T(128)} %pos_hbm.1, bf16[64,2560]{1,0:T(8,128)(2,1)} %tok_hbm.1, bf16[2560]{0:T(1024)(128)(2,1)} %an_hbm.1, bf16[1,128]{1,0:T(2,128)(2,1)} %bitcast.10, ...), custom_call_target="tpu_custom_call" | custom-call | tf_op jit(solution)/shard_map/decode_step/pallas_call | solution.py:359
  40.6 2.2 %store.1 = (bf16[64,16,8,128]{3,2,1,0:T(8,128)(2,1)}, bf16[64,16,8,128]{3,2,1,0:T(8,128)(2,1)}, bf16[64,2,8,128]{3,2,1,0:T(8,128)(2,1)}, bf16[64,2560]{1,0:T(8,128)(2,1)}) custom-call(bf16[64,16,8,128]{3,2,1,0:T(8,128)(2,1)S(1)} %bitcast.6, bf16[64,16,8,128]{3,2,1,0:T(8,128)(2,1)S(1)} %bitcast.7, bf16[64,2,8,128]{3,2,1,0:T(8,128)(2,1)S(1)} %get-tuple-element.14.refs_2_, ...), custom_call_target="tpu_custom_call" | custom-call | tf_op jit(solution)/shard_map/store/pallas_call | solution.py:396

commit v9 on v8

--- a/solution.py
+++ b/solution.py
@@ -52,23 +52,22 @@
         return (lax.axis_index("dp"), index)
 
     def tile_copy(t):
-        src, col = ((wk_hbm, 0), (wv_hbm, 0))[t] if t < 2 else (wq_hbm, (t - 2) * 512)
-        col = pl.multiple_of(core * (512 if t < 2 else 2048) + col, 512)
+        src, col = (wq_hbm, t * 512) if t < 4 else ((wk_hbm, 0), (wv_hbm, 0))[t - 4]
+        col = pl.multiple_of(core * (2048 if t < 4 else 512) + col, 512)
         return pltpu.make_async_copy(src.at[:, pl.ds(col, 512)], wbuf.at[t], wsem.at[t])
 
-    def kvload(i):
+    def kvload(i, which):
         rows = pl.ds(i * 16, 16)
-        return (pltpu.make_async_copy(kc_hbm.at[rows], kbuf.at[rows], csem.at[0, i]),
-                pltpu.make_async_copy(vc_hbm.at[rows], vbuf.at[rows], csem.at[1, i]))
+        src, dst = ((kc_hbm, kbuf), (vc_hbm, vbuf))[which]
+        return pltpu.make_async_copy(src.at[rows], dst.at[rows], csem.at[which, i])
 
     def tile_ready(t):
         tile_copy(t).wait()
         if t + DEPTH < TILES:
             tile_copy(t + DEPTH).start()
         else:
-            for i in (2 * (t + DEPTH - TILES), 2 * (t + DEPTH - TILES) + 1):
-                for c in kvload(i):
-                    c.start()
+            for i in range(4):
+                kvload(i, t + DEPTH - TILES).start()
 
     inputs = [pltpu.make_async_copy(a, b, isem.at[i]) for i, (a, b) in enumerate(
         [(tok_hbm, tok_ref), (an_hbm, an_ref), (pos_hbm, pos_ref), (freq_hbm, freq_ref), (kn_hbm, kn_ref), (qn_hbm, qn_ref)])]
@@ -113,36 +112,33 @@
         turned = normed * cosr[...] + pltpu.roll(normed, HEAD_DIM // 2, 1) * sinr[...]
         return turned.astype(BF16).astype(F32)
 
-    for t in range(2):
+    def gcopy(group, slot):
+        return pltpu.make_async_remote_copy(src_ref=gbuf.at[group], dst_ref=gbuf.at[group], send_sem=gsend.at[slot],
+                                            recv_sem=grecv.at[slot], device_id=dev(mate), device_id_type=MESH)
+
+    for t in range(4):
         tile_ready(t)
         res = project(t)
         for h in range(4):
+            gbuf[2 * core + t // 2, :, 4 * (t % 2) + h, :] = rope(res[:, h * 128:(h + 1) * 128], qn_ref[...].astype(F32))
+
+    pl.semaphore_wait(barrier, CHIPS)
+    for g in range(2):
+        gcopy(2 * core + g, g).start()
+    for t in range(2):
+        tile_ready(4 + t)
+        res = project(4 + t)
+        for h in range(4):
             head = res[:, h * 128:(h + 1) * 128]
             gbuf[4 + core, :, 4 * t + h, :] = head if t else rope(head, kn_ref[...].astype(F32))
-
-    def gcopy(group, slot):
-        return pltpu.make_async_remote_copy(src_ref=gbuf.at[group], dst_ref=gbuf.at[group], send_sem=gsend.at[slot],
-                                            recv_sem=grecv.at[slot], device_id=dev(mate), device_id_type=MESH)
-
-    for g in range(2):
-        for t2 in range(2):
-            t = 2 + g * 2 + t2
-            tile_ready(t)
-            res = project(t)
-            for h in range(4):
-                gbuf[2 * core + g, :, 4 * t2 + h, :] = rope(res[:, h * 128:(h + 1) * 128], qn_ref[...].astype(F32))
-        if g == 0:
-            pl.semaphore_wait(barrier, CHIPS)
-            gcopy(4 + core, 2).start()
-        gcopy(2 * core + g, g).start()
+    gcopy(4 + core, 2).start()
 
     wocopy = pltpu.make_async_copy(wo_hbm.at[pl.ds(pl.multiple_of(core * 2048, 2048), 2048)], wobuf, wosem.at[0])
     wocopy.start()
-    for slot in range(3):
-        gcopy(4 + core if slot == 2 else 2 * core + slot, slot).wait()
+    for g in range(2):
+        gcopy(2 * core + g, g).wait()
     for i in range(4):
-        for c in kvload(i):
-            c.wait()
+        kvload(i, 0).wait()
 
     def block_of(i):
         return lax.rem(zed + 2 + i // 2 - (i // 4) * (2 * (i // 2) - 1), 4) * 2 + lax.rem(i, 2)
@@ -220,6 +216,9 @@
                                           device_id=dev(mate), device_id_type=MESH)
     stcopy.start()
 
+    for i in range(4):
+        kvload(i, 1).wait()
+
     @pl.loop(0, LAG)
     def _(i):
         mix(i)
@@ -253,6 +252,7 @@
         return pltpu.make_async_remote_copy(src_ref=src, dst_ref=dst, send_sem=send, recv_sem=recv, device_id=dev(mate),
                                             device_id_type=MESH)
 
+    gcopy(4 + core, 2).wait()
     upper = iota((SEQS, 8, HEAD_DIM), 1) < 4
     new_ref[:, 0] = jnp.where(upper, gbuf[4], pltpu.roll(gbuf[5], 4, 1)).astype(BF16)
     new_ref[:, 1] = jnp.where(upper, pltpu.roll(gbuf[4], 4, 1), gbuf[5]).astype(BF16)

time: 43 us -> 41.9 us (0.974)
  Pallas kernels: 42.2 us -> 41.1 us
    pallas_call x1, Pallas kernels: 40 us -> 38.9 us  [step_call(): pl.pallas_call(step_kernel, name='decode_step', out_shape=(jax.ShapeDtype...]
where the time goes in v9:
time: 41.9 us; the launch traced here: 41.8 us
  Pallas kernels  41.1 us (98%)
  between operations  0.64 us (2%)
    pallas_call x1, Pallas kernels, step_call(): pl.pallas_call(step_kernel, name='decode_step', out_shape=(jax.ShapeDtype...  38.9 us
    pallas_call x1, Pallas kernels, store_call(): pl.pallas_call(store_kernel, name='store', out_shape=tuple((jax.ShapeDtyp...  2.22 us

profile of v9, /device:TPU:1, one launch (start us, length us, event | category | flops | bytes accessed | tf_op | source)
XLA Modules:
  0.0 41.8 jit_solution(2584706668216429942)
XLA Ops:
  0.6 38.9 %decode_step.1 = (bf16[64,2560]{1,0:T(8,128)(2,1)S(1)}, bf16[64,2,8,128]{3,2,1,0:T(8,128)(2,1)S(1)}, bf16[64,128,128]{2,1,0:T(8,128)(2,1)S(1)}, bf16[64,128,128]{2,1,0:T(8,128)(2,1)S(1)}) custom-call(s32[64]{0:T(128)} %pos_hbm.1, bf16[64,2560]{1,0:T(8,128)(2,1)} %tok_hbm.1, bf16[2560]{0:T(1024)(128)(2,1)} %an_hbm.1, bf16[1,128]{1,0:T(2,128)(2,1)} %bitcast.10, ...), custom_call_target="tpu_custom_call" | custom-call | tf_op jit(solution)/shard_map/decode_step/pallas_call | solution.py:359
  39.5 2.2 %store.1 = (bf16[64,16,8,128]{3,2,1,0:T(8,128)(2,1)}, bf16[64,16,8,128]{3,2,1,0:T(8,128)(2,1)}, bf16[64,2,8,128]{3,2,1,0:T(8,128)(2,1)}, bf16[64,2560]{1,0:T(8,128)(2,1)}) custom-call(bf16[64,16,8,128]{3,2,1,0:T(8,128)(2,1)S(1)} %bitcast.6, bf16[64,16,8,128]{3,2,1,0:T(8,128)(2,1)S(1)} %bitcast.7, bf16[64,2,8,128]{3,2,1,0:T(8,128)(2,1)S(1)} %get-tuple-element.14.refs_2_, ...), custom_call_target="tpu_custom_call" | custom-call | tf_op jit(solution)/shard_map/store/pallas_call | solution.py:396

commit v10 on v9

--- a/solution.py
+++ b/solution.py
@@ -235,16 +235,18 @@
         pltpu.make_async_remote_copy(src_ref=stsend.at[lax.div(s, 8)], dst_ref=rst.at[chip], send_sem=tsend.at[0], recv_sem=trecv.at[0],
                                      device_id=dev(s * 2 + core), device_id_type=MESH).start()
 
+    def mix_and_merge(first, last):
+        @pl.loop(first, last)
+        def _(i):
+            @pl.when(i < 8)
+            def _():
+                mix(i)
+
+            merge(i - LAG)
+
+    mix_and_merge(LAG, LAG + 2)
     each_other(send_stats)
-
-    @pl.loop(LAG, 8 + LAG)
-    def _(i):
-        @pl.when(i < 8)
-        def _():
-            mix(i)
-
-        merge(i - LAG)
-
+    mix_and_merge(LAG + 2, LAG + 8)
     rst[chip] = stsend[chip // 8]
     rbuf[chip] = osend[chip]
 

time: 41.9 us -> 42.3 us (level)
    pallas_call x1, Pallas kernels: 38.9 us -> 39.3 us  [step_call(): pl.pallas_call(step_kernel, name='decode_step', out_shape=(jax.ShapeDtype...]
where the time goes in v10:
time: 42.3 us; the launch traced here: 42.2 us
  Pallas kernels  41.5 us (98%)
  between operations  0.64 us (2%)
    pallas_call x1, Pallas kernels, step_call(): pl.pallas_call(step_kernel, name='decode_step', out_shape=(jax.ShapeDtype...  39.3 us
    pallas_call x1, Pallas kernels, store_call(): pl.pallas_call(store_kernel, name='store', out_shape=tuple((jax.ShapeDtyp...  2.22 us

profile of v10, /device:TPU:1, one launch (start us, length us, event | category | flops | bytes accessed | tf_op | source)
XLA Modules:
  0.0 42.2 jit_solution(6544773498660388611)
XLA Ops:
  0.6 39.3 %decode_step.1 = (bf16[64,2560]{1,0:T(8,128)(2,1)S(1)}, bf16[64,2,8,128]{3,2,1,0:T(8,128)(2,1)S(1)}, bf16[64,128,128]{2,1,0:T(8,128)(2,1)S(1)}, bf16[64,128,128]{2,1,0:T(8,128)(2,1)S(1)}) custom-call(s32[64]{0:T(128)} %pos_hbm.1, bf16[64,2560]{1,0:T(8,128)(2,1)} %tok_hbm.1, bf16[2560]{0:T(1024)(128)(2,1)} %an_hbm.1, bf16[1,128]{1,0:T(2,128)(2,1)} %bitcast.10, ...), custom_call_target="tpu_custom_call" | custom-call | tf_op jit(solution)/shard_map/decode_step/pallas_call | solution.py:361
  40.0 2.2 %store.1 = (bf16[64,16,8,128]{3,2,1,0:T(8,128)(2,1)}, bf16[64,16,8,128]{3,2,1,0:T(8,128)(2,1)}, bf16[64,2,8,128]{3,2,1,0:T(8,128)(2,1)}, bf16[64,2560]{1,0:T(8,128)(2,1)}) custom-call(bf16[64,16,8,128]{3,2,1,0:T(8,128)(2,1)S(1)} %bitcast.6, bf16[64,16,8,128]{3,2,1,0:T(8,128)(2,1)S(1)} %bitcast.7, bf16[64,2,8,128]{3,2,1,0:T(8,128)(2,1)S(1)} %get-tuple-element.14.refs_2_, ...), custom_call_target="tpu_custom_call" | custom-call | tf_op jit(solution)/shard_map/store/pallas_call | solution.py:398
